TPU v7x, 32 devices: a whole 2x2x4 slice. The times are simulated.
32 devices in a mesh: ctx: 8 (over z, y), dp: 4 (over x, core).
Axes of the slice: x: 2, y: 2, z: 4, core: 2. Of those that a mesh axis runs over, the one named last changes fastest.
Arguments:
- tokens: bfloat16 [8, 512, 4096], P('dp', 'ctx'), may hold values from -6 to 6
- queries: bfloat16 [8, 512, 2048], P('dp', 'ctx'), may hold values from -160 to 160
- d_attended: bfloat16 [8, 512, 2048], P('dp', 'ctx'), may hold values from -6 to 6
- span_order: int32 [16], replicated, may hold values from 0 to 15, each once
- norm_gain: float32 [4096], replicated, may hold values from 0.1 to 1.9
- key_weight: bfloat16 [4096, 512], replicated, may hold values from -0.09375 to 0.09375
- value_weight: bfloat16 [4096, 512], replicated, may hold values from -0.09375 to 0.09375
Outputs:
- attended: bfloat16 [8, 512, 2048], P('dp', 'ctx')
- grad_queries: bfloat16 [8, 512, 2048], P('dp', 'ctx')
- grad_tokens: bfloat16 [8, 512, 4096], P('dp', 'ctx')
- grad_key_weight: float32 [4096, 512], P(('ctx', 'dp'))
- grad_value_weight: float32 [4096, 512], P(('ctx', 'dp'))
- grad_gain: float32 [4096], P(('ctx', 'dp'))
All inputs are finite; a program needn't handle non-finite values.
Results may differ from a plain program's by a relative error of at most 0.025.
The roundings to bfloat16 on the way count: a program that leaves them out, or rounds other values in their place, can miss the bound.
Values may be sent and summed in bfloat16 or wider, within the bound.
A program may use at most 192 MiB of HBM per device.

v0:
```python
import jax
import jax.numpy as jnp
from jax import lax
from jax.sharding import PartitionSpec as P

KV_HEADS = 4
HEAD_DIM = 128


ROPE_BASE = 500000.0
EPSILON = 1e-05


def positions(span_order, span_len):
    offsets = jnp.arange(span_len, dtype=jnp.int32)
    return (span_order[:, None] * span_len + offsets[None, :]).reshape(-1)


def rotation(token_pos, head_size):
    half_dim = head_size // 2
    frequency = ROPE_BASE ** (-2.0 * jnp.arange(half_dim, dtype=jnp.float32) / head_size)
    angles = token_pos.astype(jnp.float32)[:, None] * frequency[None, :]
    angles = jnp.concatenate([angles, angles], axis=1)
    return (jnp.cos(angles), jnp.sin(angles))


def rotate_half(values):
    half_dim = values.shape[-1] // 2
    return jnp.concatenate([-values[..., half_dim:], values[..., :half_dim]], axis=-1)


def rotate_back(values):
    half_dim = values.shape[-1] // 2
    return jnp.concatenate([values[..., half_dim:], -values[..., :half_dim]], axis=-1)


def normalize(tokens, norm_gain):
    widened = tokens.astype(jnp.float32)
    rms_scale = lax.rsqrt(jnp.mean(widened * widened, axis=-1, keepdims=True) + EPSILON)
    return ((widened * rms_scale * norm_gain).astype(jnp.bfloat16), rms_scale)


def project_keys(normed, key_weight, value_weight, cosine, sine_table, kv_heads, head_size):
    row_count = normed.shape[0]
    key_pre = jnp.dot(normed, key_weight, preferred_element_type=jnp.float32).reshape(
        row_count, kv_heads, head_size
    )
    rotated = key_pre * cosine[:, None, :] + rotate_half(key_pre) * sine_table[:, None, :]
    value_rows = jnp.dot(normed, value_weight, preferred_element_type=jnp.float32)
    return (
        rotated.reshape(row_count, kv_heads * head_size).astype(jnp.bfloat16),
        value_rows.astype(jnp.bfloat16),
    )


def attend_group(query_group, grad_group, key_group, value_group, causal_mask, score_scale):
    scores = (
        jnp.einsum("tgd,sd->gts", query_group, key_group, preferred_element_type=jnp.float32)
        * score_scale
    )
    scores = jnp.where(causal_mask[None], scores, -1e30)
    row_max = jnp.max(scores, axis=-1, keepdims=True)
    exponent = jnp.exp(scores - row_max)
    probability = exponent / jnp.sum(exponent, axis=-1, keepdims=True)
    probability_b = probability.astype(jnp.bfloat16)
    attended = jnp.einsum(
        "gts,sd->tgd", probability_b, value_group, preferred_element_type=jnp.float32
    ).astype(jnp.bfloat16)
    dprob = jnp.einsum("tgd,sd->gts", grad_group, value_group, preferred_element_type=jnp.float32)
    delta = jnp.sum(grad_group.astype(jnp.float32) * attended.astype(jnp.float32), axis=-1)
    dscores = (probability * (dprob - jnp.transpose(delta)[:, :, None])).astype(jnp.bfloat16)
    dquery = (
        jnp.einsum("gts,sd->tgd", dscores, key_group, preferred_element_type=jnp.float32)
        * score_scale
    ).astype(jnp.bfloat16)
    key_term = (
        jnp.einsum("gts,tgd->sd", dscores, query_group, preferred_element_type=jnp.float32)
        * score_scale
    )
    value_term = jnp.einsum(
        "gts,tgd->sd", probability_b, grad_group, preferred_element_type=jnp.float32
    )
    return (attended, dquery, key_term, value_term)


def attend_device(queries, grads, all_keys, all_values, query_pos, key_pos, kv_heads, head_size):
    row_count = queries.shape[0]
    group_size = queries.shape[1] // (kv_heads * head_size)
    group_width = group_size * head_size
    causal_mask = key_pos[None, :] <= query_pos[:, None]
    score_scale = head_size ** (-0.5)
    outputs = []
    for head_group in range(kv_heads):
        query_group = queries[:, head_group * group_width : (head_group + 1) * group_width].reshape(
            row_count, group_size, head_size
        )
        grad_group = grads[:, head_group * group_width : (head_group + 1) * group_width].reshape(
            row_count, group_size, head_size
        )
        key_group = all_keys[:, head_group * head_size : (head_group + 1) * head_size]
        value_group = all_values[:, head_group * head_size : (head_group + 1) * head_size]
        outputs.append(
            attend_group(query_group, grad_group, key_group, value_group, causal_mask, score_scale)
        )
    attended = jnp.concatenate(
        [item[0].reshape(row_count, group_width) for item in outputs], axis=1
    )
    dquery = jnp.concatenate([item[1].reshape(row_count, group_width) for item in outputs], axis=1)
    key_terms = jnp.concatenate([item[2] for item in outputs], axis=1)
    value_terms = jnp.concatenate([item[3] for item in outputs], axis=1)
    return (attended, dquery, key_terms, value_terms)


def finish_backward(
    tokens,
    normed,
    rms_scale,
    key_grad,
    value_grad,
    cosine,
    sine_table,
    norm_gain,
    key_weight,
    value_weight,
    kv_heads,
    head_size,
):
    row_count = tokens.shape[0]
    shaped = key_grad.reshape(row_count, kv_heads, head_size)
    key_pre_grad = (
        (shaped * cosine[:, None, :] + rotate_back(shaped * sine_table[:, None, :]))
        .reshape(row_count, kv_heads * head_size)
        .astype(jnp.bfloat16)
    )
    value_pre_grad = value_grad.astype(jnp.bfloat16)
    weight_key = jnp.dot(normed.T, key_pre_grad, preferred_element_type=jnp.float32)
    weight_value = jnp.dot(normed.T, value_pre_grad, preferred_element_type=jnp.float32)
    normed_grad = jnp.dot(key_pre_grad, key_weight.T, preferred_element_type=jnp.float32) + jnp.dot(
        value_pre_grad, value_weight.T, preferred_element_type=jnp.float32
    )
    widened = tokens.astype(jnp.float32)
    gain_part = jnp.sum(normed_grad * widened * rms_scale, axis=0)
    inner_mean = jnp.mean(normed_grad * norm_gain * widened, axis=-1, keepdims=True)
    grad_rows = (
        rms_scale * norm_gain * normed_grad - widened * rms_scale**3 * inner_mean
    ).astype(jnp.bfloat16)
    return (grad_rows, weight_key, weight_value, gain_part)


def body(tokens, queries, d_attended, span_order, norm_gain, key_weight, value_weight):
    local_seqs = tokens.shape[0]
    row_count = tokens.shape[1]
    model_width = tokens.shape[2]
    kv_width = key_weight.shape[1]
    shard_index = lax.axis_index("ctx")
    token_pos = positions(span_order, row_count // 2)
    query_pos = lax.dynamic_slice_in_dim(token_pos, shard_index * row_count, row_count, 0)
    cosine, sine_table = rotation(query_pos, HEAD_DIM)
    cosine_all = jnp.tile(cosine, (local_seqs, 1))
    sine_all = jnp.tile(sine_table, (local_seqs, 1))
    flat_tokens = tokens.reshape(local_seqs * row_count, model_width)
    normed, rms_scale = normalize(flat_tokens, norm_gain)
    rotated_keys, value_rows = project_keys(
        normed, key_weight, value_weight, cosine_all, sine_all, KV_HEADS, HEAD_DIM
    )
    rotated_keys = rotated_keys.reshape(local_seqs, row_count, kv_width)
    value_rows = value_rows.reshape(local_seqs, row_count, kv_width)
    all_keys, all_values = (
        lax.all_gather(rotated_keys, "ctx", axis=1, tiled=True),
        lax.all_gather(value_rows, "ctx", axis=1, tiled=True),
    )
    attended_list, dquery_list, key_list, value_list = ([], [], [], [])
    for sequence in range(local_seqs):
        attended, dquery, key_terms, value_terms = attend_device(
            queries[sequence],
            d_attended[sequence],
            all_keys[sequence],
            all_values[sequence],
            query_pos,
            token_pos,
            KV_HEADS,
            HEAD_DIM,
        )
        attended_list.append(attended)
        dquery_list.append(dquery)
        key_list.append(key_terms)
        value_list.append(value_terms)
    key_stack = jnp.stack(key_list)
    value_stack = jnp.stack(value_list)
    key_grad, value_grad = (
        lax.psum_scatter(
            key_stack.astype(jnp.bfloat16), "ctx", scatter_dimension=1, tiled=True
        ).astype(jnp.float32),
        lax.psum_scatter(
            value_stack.astype(jnp.bfloat16), "ctx", scatter_dimension=1, tiled=True
        ).astype(jnp.float32),
    )
    key_grad = key_grad.reshape(local_seqs * row_count, kv_width)
    value_grad = value_grad.reshape(local_seqs * row_count, kv_width)
    grad_rows, weight_key, weight_value, gain_part = finish_backward(
        flat_tokens,
        normed,
        rms_scale,
        key_grad,
        value_grad,
        cosine_all,
        sine_all,
        norm_gain,
        key_weight,
        value_weight,
        KV_HEADS,
        HEAD_DIM,
    )
    weight_key, weight_value, gain_part = (
        lax.psum_scatter(
            weight_key.astype(jnp.bfloat16), "ctx", scatter_dimension=0, tiled=True
        ).astype(jnp.float32),
        lax.psum_scatter(
            weight_value.astype(jnp.bfloat16), "ctx", scatter_dimension=0, tiled=True
        ).astype(jnp.float32),
        lax.psum_scatter(
            gain_part.astype(jnp.bfloat16), "ctx", scatter_dimension=0, tiled=True
        ).astype(jnp.float32),
    )
    weight_key, weight_value, gain_part = (
        lax.psum_scatter(
            weight_key.astype(jnp.bfloat16), "dp", scatter_dimension=0, tiled=True
        ).astype(jnp.float32),
        lax.psum_scatter(
            weight_value.astype(jnp.bfloat16), "dp", scatter_dimension=0, tiled=True
        ).astype(jnp.float32),
        lax.psum_scatter(
            gain_part.astype(jnp.bfloat16), "dp", scatter_dimension=0, tiled=True
        ).astype(jnp.float32),
    )
    return (
        jnp.stack(attended_list),
        jnp.stack(dquery_list),
        grad_rows.reshape(local_seqs, row_count, model_width),
        weight_key,
        weight_value,
        gain_part,
    )


def solution(mesh):
    placed = (P("dp", "ctx", None), P("dp", "ctx", None), P("dp", "ctx", None), P(), P(), P(), P())
    return jax.shard_map(
        body,
        mesh=mesh,
        in_specs=placed,
        out_specs=(
            P("dp", "ctx", None),
            P("dp", "ctx", None),
            P("dp", "ctx", None),
            P(("ctx", "dp"), None),
            P(("ctx", "dp"), None),
            P(("ctx", "dp")),
        ),
        check_vma=False,
    )
```

profile of v0, /device:TPU:0, one launch (start us, length us, event | category | flops | bytes accessed | tf_op | source)
XLA Modules:
  0.0 512.8 jit_solution(5786807104449921285)
XLA Ops:
  7.9 1.5 fusion.8
  10.2 6.5 %copy.154 = bf16[512,4096]{1,0:T(8,128)(2,1)} copy(bf16[512,4096]{0,1:T(8,128)(2,1)} %bitcast.753) | data formatting | bytes 8388608 | tf_op jit(solution)/shard_map/dot_general | solution.py:45
  17.0 3.4 fusion.276
  21.9 3.7 convolution_convert_fusion.1
  27.7 36.9 %all-gather.5.cloned.1.call-done = bf16[2,512,512]{2,1,0:T(8,128)(2,1)} async-done(((bf16[2,64,512]{2,1,0:T(8,128)(2,1)}), bf16[2,512,512]{2,1,0:T(8,128)(2,1)}) %all-gather.5.cloned.1.call-update) | async-done | bytes 1048592 | tf_op jit(solution)/shard_map/all_gather | solution.py:169
  64.6 1.3 slice_bitcast_fusion.2
  65.9 1.7 fusion.264
  68.8 1.7 fusion.94
  70.5 35.8 %all-gather.3.cloned.1.call-done = bf16[2,512,512]{2,1,0:T(8,128)(2,1)} async-done(((bf16[2,64,512]{2,1,0:T(8,128)(2,1)}), bf16[2,512,512]{2,1,0:T(8,128)(2,1)}) %all-gather.3.cloned.1.call-update) | async-done | bytes 1048592 | tf_op jit(solution)/shard_map/all_gather | solution.py:170
  106.3 2.1 slice_bitcast_fusion.3
  108.4 1.4 multiply_reduce_fusion.4
  109.8 2.0 fusion.267
  113.6 2.4 multiply_reduce_fusion.5
  116.8 2.0 fusion.270
  120.6 2.4 multiply_reduce_fusion.6
  123.9 2.4 fusion.273
  126.3 1.2 fusion.119
  127.5 2.4 multiply_reduce_fusion.7
  130.8 2.5 fusion.252
  133.2 1.2 fusion.126
  135.3 1.4 multiply_reduce_fusion
  136.8 2.5 fusion.255
  140.5 1.4 multiply_reduce_fusion.1
  142.8 2.4 fusion.258
  146.4 1.4 multiply_reduce_fusion.2
  148.8 1.9 fusion.261
  150.7 1.2 fusion.123
  152.0 1.5 multiply_reduce_fusion.3
  153.7 1.4 fusion.71
  163.6 2.1 copy.150
  165.8 1.4 fusion.70
  168.1 2.1 copy.137
  172.1 99.3 %all-reduce.7.cloned.1.call-done = (bf16[2,512,512]{2,0,1:T(2,128)(2,1)}, bf16[2,512,512]{2,0,1:T(2,128)(2,1)}) async-done(((bf16[2,512,512]{2,0,1:T(2,128)(2,1)}, bf16[2,512,512]{2,0,1:T(2,128)(2,1)}), (bf16[2,512,512]{2,0,1:T(2,128)(2,1)}, bf16[2,512,512]{2,0,1:T(2,128)(2,1)})) %all-reduce.7.cloned.1.call-update) | async-done | bytes 2097168
  273.4 3.2 convolution_convert_fusion
  277.8 3.3 bitcast_convert_fusion
  283.7 1.8 copy.139
  288.7 1.2 fusion.107
  295.8 68.7 %reduce-scatter.5.cloned.1.call-done = bf16[512,512]{1,0:T(8,128)(2,1)} async-done(((bf16[4096,512]{1,0:T(8,128)(2,1)}), bf16[512,512]{1,0:T(8,128)(2,1)}) %reduce-scatter.5.cloned.1.call-update) | async-done | bytes 524304 | tf_op jit(solution)/shard_map/reduce_scatter | solution.py:215
  364.6 3.8 fusion.277
  368.5 1.7 fusion.18
  370.2 21.3 %all-reduce.2 = bf16[4096]{0:T(1024)(128)(2,1)S(1)} all-reduce(bf16[4096]{0:T(1024)(128)(2,1)S(1)} %get-tuple-element.6), channel_id=8, replica_groups=mesh['ctx'=8,'dp'=4] {'ctx'}, use_global_device_ids=true, to_apply=%region_33.34.clone | all-reduce | flops 4096 | bytes 16384
  391.6 6.0 %all-reduce.3 = bf16[512]{0:T(512)(128)(2,1)S(1)} all-reduce(bf16[512]{0:T(512)(128)(2,1)S(1)} %dynamic-slice.5), channel_id=9, replica_groups=mesh['ctx'=8,'dp'=4] {'dp'}, use_global_device_ids=true, to_apply=%region_34.35.clone | all-reduce | flops 512 | bytes 2048
  397.7 58.8 %reduce-scatter.9.cloned.1.call-done = bf16[512,512]{1,0:T(8,128)(2,1)} async-done(((bf16[4096,512]{1,0:T(8,128)(2,1)}), bf16[512,512]{1,0:T(8,128)(2,1)}) %reduce-scatter.9.cloned.1.call-update) | async-done | bytes 524304 | tf_op jit(solution)/shard_map/reduce_scatter | solution.py:218
  457.1 1.6 fusion.15
  458.7 21.4 %reduce-scatter.7.cloned.1.call-done = bf16[128,512]{1,0:T(8,128)(2,1)} async-done(((bf16[512,512]{1,0:T(8,128)(2,1)}), bf16[128,512]{1,0:T(8,128)(2,1)}) %reduce-scatter.7.cloned.1.call-update) | async-done | bytes 131088 | tf_op jit(solution)/shard_map/reduce_scatter | solution.py:226
  480.1 1.6 convert_element_type.361
  481.7 22.5 %reduce-scatter.11.cloned.1.call-done = bf16[128,512]{1,0:T(8,128)(2,1)} async-done(((bf16[512,512]{1,0:T(8,128)(2,1)}), bf16[128,512]{1,0:T(8,128)(2,1)}) %reduce-scatter.11.cloned.1.call-update) | async-done | bytes 131088 | tf_op jit(solution)/shard_map/reduce_scatter | solution.py:229
  504.3 1.6 convert_element_type.363
  (319 shorter events, 41.8 us)
Async XLA Ops:
  7.2 57.4 %all-gather.5.cloned.1.call-start = ((), (), s32[]{:S(2)}) async-start(), calls=%async_computation.5 | async-start | bytes 1179648 | tf_op jit(solution)/shard_map/all_gather | solution.py:169
  10.2 6.5 %copy-start = (bf16[2,64,4096]{2,1,0:T(8,128)(2,1)S(1)}, bf16[2,64,4096]{2,1,0:T(8,128)(2,1)}, u32[]{:S(2)}) copy-start(bf16[2,64,4096]{2,1,0:T(8,128)(2,1)} %param.7) | copy-start | bytes 3145732
  10.2 6.5 %copy-start.56 = (f32[4096]{0:T(1024)S(1)}, f32[4096]{0:T(1024)}, u32[]{:S(2)}) copy-start(f32[4096]{0:T(1024)} %param.11) | copy-start | bytes 49156
  21.4 84.9 %all-gather.3.cloned.1.call-start = ((), (), s32[]{:S(2)}) async-start(), calls=%async_computation.4 | async-start | bytes 1179648 | tf_op jit(solution)/shard_map/all_gather | solution.py:170
  21.6 4.0 copy-start.80
  21.9 4.0 copy-start.40
  25.6 245.8 %all-reduce.7.cloned.1.call-start = ((), (), s32[]{:S(2)}) async-start(), calls=%async_computation.10 | async-start | bytes 4194304
  26.7 39.2 %copy-start.69 = (bf16[8,4,8,128]{3,2,1,0:T(8,128)(2,1)}, bf16[8,4,8,128]{3,2,1,0:T(8,128)(2,1)S(1)}, u32[]{:S(2)}) copy-start(bf16[8,4,8,128]{3,2,1,0:T(8,128)(2,1)S(1)} %get-tuple-element.83) | copy-start | bytes 196612
  26.8 39.1 %copy-start.79 = (pred[64,512]{1,0:T(8,128)(4,1)}, pred[64,512]{1,0:T(8,128)(4,1)S(1)}, u32[]{:S(2)}) copy-start(pred[64,512]{1,0:T(8,128)(4,1)S(1)} %broadcast_compare_fusion) | copy-start | bytes 98308
  65.8 58.0 %copy-start.4 = (bf16[512,512]{1,0:T(8,128)(2,1)}, bf16[512,512]{1,0:T(8,128)(2,1)S(1)}, u32[]{:S(2)}) copy-start(bf16[512,512]{1,0:T(8,128)(2,1)S(1)} %get-tuple-element.14) | copy-start | bytes 1572868
  65.8 82.9 %copy-start.2 = (bf16[512,512]{1,0:T(8,128)(2,1)}, bf16[512,512]{1,0:T(8,128)(2,1)S(1)}, u32[]{:S(2)}) copy-start(bf16[512,512]{1,0:T(8,128)(2,1)S(1)} %get-tuple-element.15) | copy-start | bytes 1572868
  109.8 6.2 %copy-start.31 = (bf16[8,4,8,128]{3,2,1,0:T(8,128)(2,1)S(1)}, bf16[8,4,8,128]{3,2,1,0:T(8,128)(2,1)}, u32[]{:S(2)}) copy-start(bf16[8,4,8,128]{3,2,1,0:T(8,128)(2,1)} %get-tuple-element.78) | copy-start | bytes 196612
  111.8 8.8 %copy-start.29 = (bf16[8,4,8,128]{3,2,1,0:T(8,128)(2,1)S(1)}, bf16[8,4,8,128]{3,2,1,0:T(8,128)(2,1)}, u32[]{:S(2)}) copy-start(bf16[8,4,8,128]{3,2,1,0:T(8,128)(2,1)} %get-tuple-element.77) | copy-start | bytes 196612
  113.5 10.3 %copy-start.65 = (bf16[8,4,8,128]{3,2,1,0:T(8,128)(2,1)S(1)}, bf16[8,4,8,128]{3,2,1,0:T(8,128)(2,1)}, u32[]{:S(2)}) copy-start(bf16[8,4,8,128]{3,2,1,0:T(8,128)(2,1)} %get-tuple-element.84) | copy-start | bytes 196612
  118.8 8.7 %copy-start.27 = (bf16[8,4,8,128]{3,2,1,0:T(8,128)(2,1)S(1)}, bf16[8,4,8,128]{3,2,1,0:T(8,128)(2,1)}, u32[]{:S(2)}) copy-start(bf16[8,4,8,128]{3,2,1,0:T(8,128)(2,1)} %get-tuple-element.80) | copy-start | bytes 196612
  120.5 10.2 %copy-start.63 = (bf16[8,4,8,128]{3,2,1,0:T(8,128)(2,1)S(1)}, bf16[8,4,8,128]{3,2,1,0:T(8,128)(2,1)}, u32[]{:S(2)}) copy-start(bf16[8,4,8,128]{3,2,1,0:T(8,128)(2,1)} %get-tuple-element.37) | copy-start | bytes 196612
  126.3 8.1 %copy-start.25 = (bf16[8,4,8,128]{3,2,1,0:T(8,128)(2,1)S(1)}, bf16[8,4,8,128]{3,2,1,0:T(8,128)(2,1)}, u32[]{:S(2)}) copy-start(bf16[8,4,8,128]{3,2,1,0:T(8,128)(2,1)} %get-tuple-element.29) | copy-start | bytes 196612
  126.3 9.1 %copy-start.6 = (bf16[512,512]{1,0:T(8,128)(2,1)S(1)}, bf16[512,512]{1,0:T(8,128)(2,1)}, u32[]{:S(2)}) copy-start(bf16[512,512]{1,0:T(8,128)(2,1)} %get-tuple-element.13) | copy-start | bytes 1572868
  127.5 9.3 %copy-start.61 = (bf16[8,4,8,128]{3,2,1,0:T(8,128)(2,1)S(1)}, bf16[8,4,8,128]{3,2,1,0:T(8,128)(2,1)}, u32[]{:S(2)}) copy-start(bf16[8,4,8,128]{3,2,1,0:T(8,128)(2,1)} %get-tuple-element.38) | copy-start | bytes 196612
  133.2 7.2 %copy-start.23 = (bf16[8,4,8,128]{3,2,1,0:T(8,128)(2,1)S(1)}, bf16[8,4,8,128]{3,2,1,0:T(8,128)(2,1)}, u32[]{:S(2)}) copy-start(bf16[8,4,8,128]{3,2,1,0:T(8,128)(2,1)} %get-tuple-element.30) | copy-start | bytes 196612
  134.4 8.4 %copy-start.59 = (bf16[8,4,8,128]{3,2,1,0:T(8,128)(2,1)S(1)}, bf16[8,4,8,128]{3,2,1,0:T(8,128)(2,1)}, u32[]{:S(2)}) copy-start(bf16[8,4,8,128]{3,2,1,0:T(8,128)(2,1)} %get-tuple-element.39) | copy-start | bytes 196612
  139.3 7.2 %copy-start.21 = (bf16[8,4,8,128]{3,2,1,0:T(8,128)(2,1)S(1)}, bf16[8,4,8,128]{3,2,1,0:T(8,128)(2,1)}, u32[]{:S(2)}) copy-start(bf16[8,4,8,128]{3,2,1,0:T(8,128)(2,1)} %get-tuple-element.31) | copy-start | bytes 196612
  140.4 8.3 %copy-start.57 = (bf16[8,4,8,128]{3,2,1,0:T(8,128)(2,1)S(1)}, bf16[8,4,8,128]{3,2,1,0:T(8,128)(2,1)}, u32[]{:S(2)}) copy-start(bf16[8,4,8,128]{3,2,1,0:T(8,128)(2,1)} %get-tuple-element.36) | copy-start | bytes 196612
  145.2 6.7 %copy-start.20 = (bf16[8,4,8,128]{3,2,1,0:T(8,128)(2,1)S(1)}, bf16[8,4,8,128]{3,2,1,0:T(8,128)(2,1)}, u32[]{:S(2)}) copy-start(bf16[8,4,8,128]{3,2,1,0:T(8,128)(2,1)} %get-tuple-element.28) | copy-start | bytes 196612
  150.7 4.4 copy-start.70
  150.7 5.3 %copy-start.8 = (bf16[512,512]{1,0:T(8,128)(2,1)S(1)}, bf16[512,512]{1,0:T(8,128)(2,1)}, u32[]{:S(2)}) copy-start(bf16[512,512]{1,0:T(8,128)(2,1)} %copy-done.7) | copy-start | bytes 1572868
  150.7 5.3 %copy-start.32 = (bf16[8,4,8,128]{3,2,1,0:T(8,128)(2,1)S(1)}, bf16[8,4,8,128]{3,2,1,0:T(8,128)(2,1)}, u32[]{:S(2)}) copy-start(bf16[8,4,8,128]{3,2,1,0:T(8,128)(2,1)} %get-tuple-element.78) | copy-start | bytes 196612
  150.7 5.3 %copy-start.34 = (f32[4,64,512]{2,1,0:T(8,128)S(1)}, f32[4,64,512]{2,1,0:T(8,128)}, u32[]{:S(2)}) copy-start(f32[4,64,512]{2,1,0:T(8,128)} %get-tuple-element.55) | copy-start | bytes 1572868
  150.7 5.3 %copy-start.84 = (f32[4,64]{1,0:T(4,128)S(1)}, f32[4,64]{1,0:T(4,128)}, u32[]{:S(2)}) copy-start(f32[4,64]{1,0:T(4,128)} %copy-done.83) | copy-start | bytes 3076
  150.7 5.3 %copy-start.85 = (f32[64,4]{0,1:T(4,128)S(1)}, f32[64,4]{0,1:T(4,128)}, u32[]{:S(2)}) copy-start(f32[64,4]{0,1:T(4,128)} %get-tuple-element.70) | copy-start | bytes 3076
  170.2 194.3 %reduce-scatter.5.cloned.1.call-start = ((), (), s32[]{:S(2)}) async-start(), calls=%async_computation.6 | async-start | bytes 4718592 | tf_op jit(solution)/shard_map/reduce_scatter | solution.py:215
  276.7 179.8 %reduce-scatter.9.cloned.1.call-start = ((), (), s32[]{:S(2)}) async-start(), calls=%async_computation.8 | async-start | bytes 4718592 | tf_op jit(solution)/shard_map/reduce_scatter | solution.py:218
  281.1 5.0 copy-start.81
  281.1 5.6 %copy-start.5 = (bf16[512,512]{1,0:T(8,128)(2,1)S(1)}, bf16[512,512]{1,0:T(8,128)(2,1)}, u32[]{:S(2)}) copy-start(bf16[512,512]{1,0:T(8,128)(2,1)} %copy-done.4) | copy-start | bytes 1572868
  281.1 5.8 %copy-start.10 = (bf16[4,64,512]{2,1,0:T(8,128)(2,1)S(1)}, bf16[4,64,512]{2,1,0:T(8,128)(2,1)}, u32[]{:S(2)}) copy-start(bf16[4,64,512]{2,1,0:T(8,128)(2,1)} %copy-done.9) | copy-start | bytes 786436
  281.1 6.1 %copy-start.12 = (bf16[4,64,512]{2,1,0:T(8,128)(2,1)S(1)}, bf16[4,64,512]{2,1,0:T(8,128)(2,1)}, u32[]{:S(2)}) copy-start(bf16[4,64,512]{2,1,0:T(8,128)(2,1)} %copy-done.11) | copy-start | bytes 786436
  281.1 7.6 %copy-start.3 = (bf16[512,512]{1,0:T(8,128)(2,1)S(1)}, bf16[512,512]{1,0:T(8,128)(2,1)}, u32[]{:S(2)}) copy-start(bf16[512,512]{1,0:T(8,128)(2,1)} %copy-done.2) | copy-start | bytes 1572868
  281.1 199.0 %reduce-scatter.7.cloned.1.call-start = ((), (), s32[]{:S(2)}) async-start(), calls=%async_computation.7 | async-start | bytes 655360 | tf_op jit(solution)/shard_map/reduce_scatter | solution.py:226
  286.9 6.6 %copy-start.71 = (bf16[128,4,64]{0,2,1:T(8,128)(2,1)S(1)}, bf16[128,4,64]{0,2,1:T(8,128)(2,1)}, u32[]{:S(2)}) copy-start(bf16[128,4,64]{0,2,1:T(8,128)(2,1)} %get-tuple-element.69) | copy-start | bytes 196612
  286.9 6.7 %copy-start.72 = (bf16[128,4,64]{0,2,1:T(8,128)(2,1)S(1)}, bf16[128,4,64]{0,2,1:T(8,128)(2,1)}, u32[]{:S(2)}) copy-start(bf16[128,4,64]{0,2,1:T(8,128)(2,1)} %get-tuple-element.71) | copy-start | bytes 196612
  286.9 6.7 %copy-start.73 = (bf16[128,4,64]{0,2,1:T(8,128)(2,1)S(1)}, bf16[128,4,64]{0,2,1:T(8,128)(2,1)}, u32[]{:S(2)}) copy-start(bf16[128,4,64]{0,2,1:T(8,128)(2,1)} %get-tuple-element.73) | copy-start | bytes 196612
  287.2 6.5 %copy-start.74 = (bf16[128,4,64]{0,2,1:T(8,128)(2,1)S(1)}, bf16[128,4,64]{0,2,1:T(8,128)(2,1)}, u32[]{:S(2)}) copy-start(bf16[128,4,64]{0,2,1:T(8,128)(2,1)} %get-tuple-element.75) | copy-start | bytes 196612
  287.2 6.5 %copy-start.75 = (bf16[128,4,64]{0,2,1:T(8,128)(2,1)S(1)}, bf16[128,4,64]{0,2,1:T(8,128)(2,1)}, u32[]{:S(2)}) copy-start(bf16[128,4,64]{0,2,1:T(8,128)(2,1)} %get-tuple-element.61) | copy-start | bytes 196612
  287.2 6.5 %copy-start.76 = (bf16[128,4,64]{0,2,1:T(8,128)(2,1)S(1)}, bf16[128,4,64]{0,2,1:T(8,128)(2,1)}, u32[]{:S(2)}) copy-start(bf16[128,4,64]{0,2,1:T(8,128)(2,1)} %get-tuple-element.63) | copy-start | bytes 196612
  287.2 6.5 %copy-start.77 = (bf16[128,4,64]{0,2,1:T(8,128)(2,1)S(1)}, bf16[128,4,64]{0,2,1:T(8,128)(2,1)}, u32[]{:S(2)}) copy-start(bf16[128,4,64]{0,2,1:T(8,128)(2,1)} %get-tuple-element.65) | copy-start | bytes 196612
  287.5 6.3 %copy-start.78 = (bf16[128,4,64]{0,2,1:T(8,128)(2,1)S(1)}, bf16[128,4,64]{0,2,1:T(8,128)(2,1)}, u32[]{:S(2)}) copy-start(bf16[128,4,64]{0,2,1:T(8,128)(2,1)} %get-tuple-element.67) | copy-start | bytes 196612
  364.6 139.7 %reduce-scatter.11.cloned.1.call-start = ((), (), s32[]{:S(2)}) async-start(), calls=%async_computation.9 | async-start | bytes 655360 | tf_op jit(solution)/shard_map/reduce_scatter | solution.py:229
  368.5 88.6 %copy-start.98 = (f32[128]{0:T(128)S(1)}, f32[128]{0:T(128)}, u32[]{:S(2)}) copy-start(f32[128]{0:T(128)} %multiply_multiply_fusion) | copy-start | bytes 1540
  (60 other events, 118.6 us)
Sparse Core Ops, SparseCore 0:
  21.6 42.9 all-gather.4
  67.3 38.9 all-gather.2
  170.3 101.0 all-reduce.6
  276.8 87.6 reduce-scatter.4
  368.0 88.4 reduce-scatter.8
  458.8 21.2 reduce-scatter.6
  482.6 21.6 reduce-scatter.10
where the time goes:
time: 514 us; the launch traced here: 513 us
  waiting for transfers between devices  344 us (67%)
  matrix products  75.4 us (15%)
  blocking collectives  27.4 us (5%)
  local copies, waits for them, and re-layouts  26.2 us (5%)
  other arithmetic  21.8 us (4%)
  between operations  17.6 us (3%)
    unnamed x8, waiting for transfers between devices  99.4 us
    reduce_scatter x1, waiting for transfers between devices, body(): lax.psum_scatter(weight_key.astype(jnp.bfloat16), 'ctx', scatter_dimensio...  68.7 us
    reduce_scatter x1, waiting for transfers between devices, body(): lax.psum_scatter(weight_value.astype(jnp.bfloat16), 'ctx', scatter_dimens...  58.8 us
    all_gather x1, waiting for transfers between devices, body(): lax.all_gather(rotated_keys, 'ctx', axis=1, tiled=True)  36.9 us
    all_gather x1, waiting for transfers between devices, body(): lax.all_gather(value_rows, 'ctx', axis=1, tiled=True)  35.8 us
    unnamed x2, blocking collectives  27.4 us
    reduce_scatter x1, waiting for transfers between devices, body(): lax.psum_scatter(weight_value.astype(jnp.bfloat16), 'dp', scatter_dimensi...  22.5 us
    reduce_scatter x1, waiting for transfers between devices, body(): lax.psum_scatter(weight_key.astype(jnp.bfloat16), 'dp', scatter_dimension...  21.4 us
  transfers between devices with their start and end apart: 7, of which 7 were waited for; matrix products, arithmetic and copies ran while one was open for 8% of the time, Pallas kernels for 0%

commit v1 on v0

v1 whole, which is shorter than its diff:
```python
import functools

import jax
import jax.numpy as jnp
from jax import lax
from jax.experimental import pallas as pl
from jax.experimental.pallas import tpu as pltpu
from jax.sharding import PartitionSpec as P

KV_HEADS = 4
HEAD_DIM = 128
ROPE_BASE = 500000.0
EPSILON = 1e-05
MESH = pl.DeviceIdType.MESH
VMEM = pl.BlockSpec(memory_space=pltpu.VMEM)
F32 = jnp.float32
BF16 = jnp.bfloat16
LIMIT = 60 * 1024 * 1024


def positions(span_order, span_len):
    offsets = jnp.arange(span_len, dtype=jnp.int32)
    return (span_order[:, None] * span_len + offsets[None, :]).reshape(-1)


def rotation(token_pos, head_size):
    half_dim = head_size // 2
    frequency = ROPE_BASE ** (-2.0 * jnp.arange(half_dim, dtype=F32) / head_size)
    angles = token_pos.astype(F32)[:, None] * frequency[None, :]
    angles = jnp.concatenate([angles, angles], axis=1)
    return (jnp.cos(angles), jnp.sin(angles))


def ring_place(index, n):
    return jnp.where(index % 2 == 0, index // 2, n - 1 - index // 2)


def ring_index(place, n):
    place = (place + 2 * n) % n
    return jnp.where(place < n // 2, 2 * place, 2 * (n - 1 - place) + 1)


def remote(src, dst, send, recv, axis, target):
    return pltpu.make_async_remote_copy(
        src_ref=src,
        dst_ref=dst,
        send_sem=send,
        recv_sem=recv,
        device_id={axis: target},
        device_id_type=MESH,
    )


def greet(axis, n, me):
    barrier = pltpu.get_barrier_semaphore()
    for j in range(1, n):
        pl.semaphore_signal(
            barrier, inc=1, device_id={axis: (me + j) % n}, device_id_type=MESH
        )
    pl.semaphore_wait(barrier, n - 1)


def ring_gather(n, me, firsts, alls, send, recv, extra=None):
    place = ring_place(me, n)
    sign = (1, -1)
    targets = [ring_index(place + 1, n), ring_index(place - 1, n)]
    chunks = firsts[0].shape[0]

    def copy(d, c, s, first=False):
        owner = ring_index(place - sign[d] * s, n)
        src = firsts[d].at[c] if first else alls[d].at[owner, c]
        return remote(
            src, alls[d].at[owner, c], send.at[d, c, s], recv.at[d, c, s], "ctx", targets[d]
        )

    def arrive(d, c, s):
        owner = ring_index(place - sign[d] * (s + 1), n)
        slot = alls[d].at[owner, c]
        remote(slot, slot, send.at[d, c, s], recv.at[d, c, s], "ctx", targets[d]).wait_recv()

    for c in range(chunks):
        for d in range(2):
            copy(d, c, 0, first=True).start()

    def step(s, carry):
        for c in range(chunks):
            for d in range(2):
                arrive(d, c, s)
                copy(d, c, s + 1).start()
        if extra is not None:
            extra(s + 1)
        return carry

    if extra is not None:
        extra(0)
    lax.fori_loop(0, n - 2, step, 0)
    for c in range(chunks):
        for d in range(2):
            arrive(d, c, n - 2)

    def drain(s, carry):
        for c in range(chunks):
            for d in range(2):
                copy(d, c, s).wait_send()
        return carry

    lax.fori_loop(0, n - 1, drain, 0)


def gather_kernel(n, k_ref, v_ref, a_ref, gk, gv, ga, send, recv, asend, arecv):
    me = lax.axis_index("ctx")
    width = ga.shape[2]
    greet("ctx", n, me)
    gk[me] = k_ref[...]
    gv[me] = v_ref[...]
    ga[me] = a_ref[:, pl.ds(pl.multiple_of(me * width, 128), width)]

    def piece(j):
        target = (me + j) % n
        return remote(
            a_ref.at[:, pl.ds(pl.multiple_of(target * width, 128), width)],
            ga.at[me],
            asend.at[j - 1],
            arecv.at[j - 1],
            "ctx",
            target,
        )

    ring_gather(n, me, (k_ref, v_ref), (gk, gv), send, recv, lambda s: piece(s + 1).start())

    def finish(j, carry):
        piece(j).wait_send()
        slot = ga.at[(me + n - j) % n]
        remote(slot, slot, asend.at[j - 1], arecv.at[j - 1], "ctx", (me + j) % n).wait_recv()
        return carry

    lax.fori_loop(1, n, finish, 0)


def gather(n, keys, values, normed):
    seqs = keys.shape[0]
    kv = jax.ShapeDtypeStruct((n,) + keys.shape, BF16)
    return pl.pallas_call(
        functools.partial(gather_kernel, n),
        out_shape=(
            kv,
            kv,
            jax.ShapeDtypeStruct((n, normed.shape[0], normed.shape[1] // n), BF16),
        ),
        in_specs=[VMEM] * 3,
        out_specs=[VMEM] * 3,
        scratch_shapes=[
            pltpu.SemaphoreType.DMA((2, seqs, n - 1)),
            pltpu.SemaphoreType.DMA((2, seqs, n - 1)),
            pltpu.SemaphoreType.DMA((n - 1,)),
            pltpu.SemaphoreType.DMA((n - 1,)),
        ],
        compiler_params=pltpu.CompilerParams(
            collective_id=0, has_side_effects=True, vmem_limit_bytes=LIMIT
        ),
        name="gather_kv",
    )(keys, values, normed)


def attention_kernel(q_ref, g_ref, k_ref, v_ref, qpos_ref, kpos_ref, att, dq, dk, dv):
    n, _, rows, head = k_ref.shape
    group = q_ref.shape[2] // head
    scale = head ** (-0.5)
    query = jnp.concatenate([q_ref[0, :, i * head : (i + 1) * head] for i in range(group)], axis=0)
    grad = jnp.concatenate([g_ref[0, :, i * head : (i + 1) * head] for i in range(group)], axis=0)
    key = k_ref[...].reshape(n * rows, head)
    value = v_ref[...].reshape(n * rows, head)
    nt = (((1,), (1,)), ((), ()))
    nn = (((1,), (0,)), ((), ()))
    tn = (((0,), (0,)), ((), ()))
    dot = functools.partial(lax.dot_general, preferred_element_type=F32)
    keep = kpos_ref[...] <= jnp.concatenate([qpos_ref[...]] * group, axis=0)
    scores = jnp.where(keep, dot(query, key, nt) * scale, -1e30)
    exponent = jnp.exp(scores - jnp.max(scores, axis=1, keepdims=True))
    probability = exponent * (1.0 / jnp.sum(exponent, axis=1, keepdims=True))
    rounded = probability.astype(BF16)
    attended = dot(rounded, value, nn).astype(BF16)
    delta = jnp.sum(grad.astype(F32) * attended.astype(F32), axis=1, keepdims=True)
    dscores = (probability * (dot(grad, value, nt) - delta)).astype(BF16)
    dquery = (dot(dscores, key, nn) * scale).astype(BF16)
    for i in range(group):
        att[0, :, i * head : (i + 1) * head] = attended[i * rows : (i + 1) * rows]
        dq[0, :, i * head : (i + 1) * head] = dquery[i * rows : (i + 1) * rows]
    dk[...] = (dot(dscores, query, tn) * scale).astype(BF16).reshape(n, 1, rows, head)
    dv[...] = dot(rounded, grad, tn).astype(BF16).reshape(n, 1, rows, head)


def attention(queries, grads, all_keys, all_values, query_pos, key_pos):
    n, seqs, rows, width = all_keys.shape
    kv_heads = width // HEAD_DIM
    wide = pl.BlockSpec((1, rows, queries.shape[2] // kv_heads), lambda s, h: (s, 0, h))
    narrow = pl.BlockSpec((n, 1, rows, HEAD_DIM), lambda s, h: (0, s, 0, h))
    return pl.pallas_call(
        attention_kernel,
        grid=(seqs, kv_heads),
        out_shape=(
            jax.ShapeDtypeStruct(queries.shape, BF16),
            jax.ShapeDtypeStruct(queries.shape, BF16),
            jax.ShapeDtypeStruct(all_keys.shape, BF16),
            jax.ShapeDtypeStruct(all_keys.shape, BF16),
        ),
        in_specs=[
            wide,
            wide,
            narrow,
            narrow,
            pl.BlockSpec((rows, 1), lambda s, h: (0, 0)),
            pl.BlockSpec((1, n * rows), lambda s, h: (0, 0)),
        ],
        out_specs=[wide, wide, narrow, narrow],
        compiler_params=pltpu.CompilerParams(vmem_limit_bytes=LIMIT),
        name="attention",
    )(queries, grads, all_keys, all_values, query_pos[:, None], key_pos[None, :])


def reduce_kernel(n, dk, dv, cos_ref, sin_ref, gk, gv, ik, iv, own_k, own_v, rs, rr, send, recv):
    me = lax.axis_index("ctx")
    place = ring_place(me, n)
    seqs = dk.shape[1]
    sign = (1, -1)
    targets = [ring_index(place + 1, n), ring_index(place - 1, n)]
    terms = (dk, dv)
    inbox = (ik, iv)
    greet("ctx", n, me)

    def copy(d, c, s, first=False):
        src = terms[d].at[targets[1 - d], c] if first else inbox[d].at[s - 1, c]
        return remote(src, inbox[d].at[s, c], rs.at[d, c, s], rr.at[d, c, s], "ctx", targets[d])

    def total(d, c, s):
        slot = inbox[d].at[s, c]
        remote(slot, slot, rs.at[d, c, s], rr.at[d, c, s], "ctx", targets[d]).wait_recv()
        owner = ring_index(place - sign[d] * (s + 2), n)
        return inbox[d][s, c].astype(F32) + terms[d][owner, c].astype(F32)

    for c in range(seqs):
        for d in range(2):
            copy(d, c, 0, first=True).start()

    def step(s, carry):
        for c in range(seqs):
            for d in range(2):
                inbox[d][s, c] = total(d, c, s).astype(BF16)
                copy(d, c, s + 1).start()
        return carry

    lax.fori_loop(0, n - 2, step, 0)
    for c in range(seqs):
        key_grad = total(0, c, n - 2)
        for h in range(key_grad.shape[1] // HEAD_DIM):
            part = key_grad[:, h * HEAD_DIM : (h + 1) * HEAD_DIM]
            turned = pltpu.roll(part, HEAD_DIM // 2, 1)
            back = (part * cos_ref[...] + turned * sin_ref[...]).astype(BF16)
            own_k[c, :, h * HEAD_DIM : (h + 1) * HEAD_DIM] = back
        own_v[c] = total(1, c, n - 2).astype(BF16)
    gk[me] = own_k[...]
    gv[me] = own_v[...]
    ring_gather(n, me, (own_k, own_v), (gk, gv), send, recv)

    def drain(s, carry):
        for c in range(seqs):
            for d in range(2):
                slot = inbox[d].at[s, c]
                remote(slot, slot, rs.at[d, c, s], rr.at[d, c, s], "ctx", targets[d]).wait_send()
        return carry

    lax.fori_loop(0, n - 1, drain, 0)


def reduce_gather(n, key_terms, value_terms, cosine, sine_back):
    _, seqs, rows, width = key_terms.shape
    kv = jax.ShapeDtypeStruct(key_terms.shape, BF16)
    sems = pltpu.SemaphoreType.DMA((2, seqs, n - 1))
    return pl.pallas_call(
        functools.partial(reduce_kernel, n),
        out_shape=(kv, kv),
        in_specs=[VMEM] * 4,
        out_specs=[VMEM] * 2,
        scratch_shapes=[
            pltpu.VMEM((n - 1, seqs, rows, width), BF16),
            pltpu.VMEM((n - 1, seqs, rows, width), BF16),
            pltpu.VMEM((seqs, rows, width), BF16),
            pltpu.VMEM((seqs, rows, width), BF16),
            sems,
            sems,
            sems,
            sems,
        ],
        compiler_params=pltpu.CompilerParams(
            collective_id=1, has_side_effects=True, vmem_limit_bytes=LIMIT
        ),
        name="reduce_kv",
    )(key_terms, value_terms, cosine, sine_back)


def scatter_kernel(m, part, out, near, held, far, send, recv):
    me = lax.axis_index("dp")
    greet("dp", m, me)
    half = m // 2
    pair = me + 1 - 2 * (me % 2)

    def first(j):
        to = (me // 2 + j) % half
        return remote(
            part.at[2 * to + pair % 2], near.at[j], send.at[j], recv.at[j], "dp", pair
        )

    def second(j):
        to = 2 * ((me // 2 + j) % half) + me % 2
        at = half + j - 1
        return remote(held.at[j - 1], far.at[j - 1], send.at[at], recv.at[at], "dp", to)

    order = list(range(1, half)) + [0]
    for j in order:
        first(j).start()
    for j in order:
        to = (me // 2 + j) % half
        first(j).wait_recv()
        both = part[2 * to + me % 2].astype(F32) + near[j].astype(F32)
        if j:
            held[j - 1] = both.astype(BF16)
            second(j).start()
        else:
            out[...] = both
    for j in range(1, half):
        second(j).wait_recv()
        out[...] += far[j - 1].astype(F32)
    for j in range(half):
        first(j).wait_send()
    for j in range(1, half):
        second(j).wait_send()


def scatter(m, part):
    _, rows, width = part.shape
    half = m // 2
    return pl.pallas_call(
        functools.partial(scatter_kernel, m),
        out_shape=jax.ShapeDtypeStruct((rows, width), F32),
        in_specs=[VMEM],
        out_specs=VMEM,
        scratch_shapes=[
            pltpu.VMEM((half, rows, width), BF16),
            pltpu.VMEM((max(half - 1, 1), rows, width), BF16),
            pltpu.VMEM((max(half - 1, 1), rows, width), BF16),
            pltpu.SemaphoreType.DMA((2 * half,)),
            pltpu.SemaphoreType.DMA((2 * half,)),
        ],
        compiler_params=pltpu.CompilerParams(
            collective_id=2, has_side_effects=True, vmem_limit_bytes=LIMIT
        ),
        name="scatter_weights",
    )(part)


def body(n, m, tokens, queries, d_attended, span_order, norm_gain, key_weight, value_weight):
    seqs, rows, model_width = tokens.shape
    kv_width = key_weight.shape[1]
    me = lax.axis_index("ctx")
    dp = lax.axis_index("dp")
    token_pos = positions(span_order, rows // 2)
    query_pos = lax.dynamic_slice_in_dim(token_pos, me * rows, rows, 0)
    cosine, sine = rotation(query_pos, HEAD_DIM)
    signs = jnp.where(jnp.arange(HEAD_DIM) < HEAD_DIM // 2, -1.0, 1.0).astype(F32)
    flat = tokens.reshape(seqs * rows, model_width)
    widened = flat.astype(F32)
    rms_scale = lax.rsqrt(jnp.mean(widened * widened, axis=-1, keepdims=True) + EPSILON)
    normed = (widened * rms_scale * norm_gain).astype(BF16)
    key_pre = jnp.dot(normed, key_weight, preferred_element_type=F32)
    key_pre = key_pre.reshape(seqs, rows, kv_width // HEAD_DIM, HEAD_DIM)
    turned = jnp.roll(key_pre, HEAD_DIM // 2, axis=-1)
    keys = key_pre * cosine[None, :, None, :] + turned * (sine * signs)[None, :, None, :]
    keys = keys.reshape(seqs, rows, kv_width).astype(BF16)
    values = jnp.dot(normed, value_weight, preferred_element_type=F32)
    values = values.reshape(seqs, rows, kv_width).astype(BF16)

    all_keys, all_values, slices = gather(n, keys, values, normed)
    attended, dquery, key_terms, value_terms = attention(
        queries, d_attended, all_keys, all_values, query_pos, token_pos
    )
    key_back, value_back = reduce_gather(n, key_terms, value_terms, cosine, -sine * signs)

    own_key = lax.dynamic_index_in_dim(key_back, me, 0, False).reshape(seqs * rows, kv_width)
    own_value = lax.dynamic_index_in_dim(value_back, me, 0, False).reshape(seqs * rows, kv_width)
    normed_grad = jnp.dot(own_key, key_weight.T, preferred_element_type=F32) + jnp.dot(
        own_value, value_weight.T, preferred_element_type=F32
    )
    inner_mean = jnp.mean(normed_grad * norm_gain * widened, axis=-1, keepdims=True)
    grad_rows = (
        rms_scale * norm_gain * normed_grad - widened * rms_scale**3 * inner_mean
    ).astype(BF16)

    stacked = slices.reshape(n * seqs * rows, model_width // n)
    weight_key = jnp.dot(
        stacked.T, key_back.reshape(n * seqs * rows, kv_width), preferred_element_type=F32
    )
    weight_value = jnp.dot(
        stacked.T, value_back.reshape(n * seqs * rows, kv_width), preferred_element_type=F32
    )
    own_rows = model_width // (n * m)
    part = jnp.concatenate([weight_key.astype(BF16), weight_value.astype(BF16)], axis=1)
    summed = scatter(m, part.reshape(m, own_rows, 2 * kv_width))
    grad_key_weight = summed[:, :kv_width]
    grad_value_weight = summed[:, kv_width:]
    start = (me * m + dp) * own_rows
    own_kw = lax.dynamic_slice_in_dim(key_weight, start, own_rows, 0).astype(F32)
    own_vw = lax.dynamic_slice_in_dim(value_weight, start, own_rows, 0).astype(F32)
    gain = lax.dynamic_slice_in_dim(norm_gain, start, own_rows, 0)
    grad_gain = jnp.sum(own_kw * grad_key_weight + own_vw * grad_value_weight, axis=1) / gain
    return (
        attended,
        dquery,
        grad_rows.reshape(seqs, rows, model_width),
        grad_key_weight,
        grad_value_weight,
        grad_gain,
    )


def solution(mesh):
    split = P("dp", "ctx", None)
    return jax.shard_map(
        functools.partial(body, mesh.shape["ctx"], mesh.shape["dp"]),
        mesh=mesh,
        in_specs=(split, split, split, P(), P(), P(), P()),
        out_specs=(
            split,
            split,
            split,
            P(("ctx", "dp"), None),
            P(("ctx", "dp"), None),
            P(("ctx", "dp")),
        ),
        check_vma=False,
    )
```

time: 514 us -> 176 us (0.34)
  waiting for transfers between devices: 344 us -> 0 us
  Pallas kernels: 0 us -> 139 us
  matrix products: 75.4 us -> 15.6 us
  blocking collectives: 27.4 us -> 0 us
  between operations: 17.6 us -> 0.8 us
  local copies, waits for them, and re-layouts: 26.2 us -> 10.4 us
  other arithmetic: 21.8 us -> 9.63 us
    reduce_scatter x4 -> x0, waiting for transfers between devices: 171 us -> none  [the longest x1 68.7 us: body(): lax.psum_scatter(weight_key.astype(jnp.bfloat16), 'ctx', scatter_dimensio...]
    pallas_call x0 -> x4, Pallas kernels: none -> 139 us  [the longest x1 64.5 us: reduce_gather(): pl.pallas_call(functools.partial(reduce_kernel, n), out_shape=(kv, kv), i...]
    unnamed x8 -> x0, waiting for transfers between devices: 99.4 us -> none
    all_gather x2 -> x0, waiting for transfers between devices: 72.7 us -> none  [the longest x1 36.9 us: body(): lax.all_gather(rotated_keys, 'ctx', axis=1, tiled=True)]
    dot_general x46 -> x6, matrix products: 58 us -> 15.6 us  [the longest x1 3.81 us: body(): jnp.dot(own_key, key_weight.T, preferred_element_type=F32)]
    unnamed x2 -> x0, blocking collectives: 27.4 us -> none
    sub x8 -> x0, matrix products: 17.4 us -> none  [attend_group(): exponent = jnp.exp(scores - row_max)]
    convert_element_type x19 -> x3, other arithmetic: 16.5 us -> 3.69 us  [the longest x1 1.59 us: body(): grad_rows = (rms_scale * norm_gain * normed_grad - widened * rms_scale **...]
  transfers between devices with their start and end apart: 7 -> 0, of which waited for: 7 -> 0; matrix products, arithmetic and copies ran while one was open for 8% -> 0% of each run, Pallas kernels for 0% -> 0%
where the time goes in v1:
time: 176 us; the launch traced here: 175 us
  Pallas kernels  139 us (79%)
  matrix products  15.6 us (9%)
  local copies, waits for them, and re-layouts  10.4 us (6%)
  other arithmetic  9.63 us (5%)
    pallas_call x1, Pallas kernels, reduce_gather(): pl.pallas_call(functools.partial(reduce_kernel, n), out_shape=(kv, kv), i...  64.5 us
    pallas_call x1, Pallas kernels, gather(): pl.pallas_call(functools.partial(gather_kernel, n), out_shape=(kv, kv, ja...  51.5 us
    pallas_call x1, Pallas kernels, scatter(): pl.pallas_call(functools.partial(scatter_kernel, m), out_shape=jax.ShapeD...  12.2 us
    pallas_call x1, Pallas kernels, attention(): pl.pallas_call(attention_kernel, grid=(seqs, kv_heads), out_shape=(jax.Sh...  10.6 us
    dot_general x1, local copies, waits for them, and re-layouts, body(): key_pre = jnp.dot(normed, key_weight, preferred_element_type=F32)  6.53 us
    dot_general x1, matrix products, body(): jnp.dot(own_key, key_weight.T, preferred_element_type=F32)  3.81 us
    dot_general x1, matrix products, body(): key_pre = jnp.dot(normed, key_weight, preferred_element_type=F32)  3.72 us
    dot_general x1, matrix products, body(): values = jnp.dot(normed, value_weight, preferred_element_type=F32)  3.61 us

profile of v1, /device:TPU:0, one launch (start us, length us, event | category | flops | bytes accessed | tf_op | source)
XLA Modules:
  0.0 175.3 jit_solution(790240087383013185)
XLA Ops:
  0.6 0.7 broadcast_multiply_fusion.2
  1.3 0.1 iota_add_fusion
  1.4 0.1 add.73
  1.5 0.1 dynamic-slice_bitcast_fusion
  1.5 0.1 broadcast_multiply_fusion
  1.6 0.8 negate_multiply_fusion
  2.5 0.0 copy-start.2
  2.5 1.5 fusion.2
  4.0 0.0 copy-start
  4.0 0.0 copy-start.3
  4.0 6.5 %copy.18 = bf16[512,4096]{1,0:T(8,128)(2,1)} copy(bf16[512,4096]{0,1:T(8,128)(2,1)} %bitcast.53) | data formatting | bytes 8388608 | tf_op jit(solution)/shard_map/dot_general | solution.py:374
  10.5 0.0 copy-done
  10.5 0.0 copy-done.3
  10.5 3.7 %fusion.14 = f32[2,64,4,128]{3,1,2,0:T(8,128)S(1)} fusion(bf16[4,128,4096,1]{2,1,0,3:T(8,128)(2,1)} %bitcast.54, bf16[2,64,4096]{2,1,0:T(8,128)(2,1)S(1)} %copy-done, f32[4096]{0:T(1024)S(1)} %copy-done.3, f32[2,64]{1,0:T(2,128)S(1)} %add_rsqrt_fusion), kind=kOutput, calls=%fused_computation.21 | convolution fusion | flops 538968064 | bytes 5521920 | tf_op jit(solution)/shard_map/dot_general | solution.py:374
  14.3 0.1 fusion.24
  14.4 0.0 copy-done.2
  14.4 0.8 copy_bitcast_fusion.k_ref
  15.2 0.1 rsqrt.16
  15.3 1.3 fusion.6.a_ref
  16.6 3.6 %fusion.11.v_ref = bf16[2,64,512]{2,1,0:T(8,128)(2,1)} fusion(bf16[4096,512]{1,0:T(8,128)(2,1)} %param.13, bf16[2,64,4096]{2,1,0:T(8,128)(2,1)S(1)} %copy-done, f32[4096]{0:T(1024)S(1)} %copy-done.3, f32[2,64]{1,0:T(2,128)S(1)} %add_rsqrt_fusion), kind=kOutput, calls=%fused_computation.19 | convolution fusion | flops 539033600 | bytes 5390848 | tf_op jit(solution)/shard_map/dot_general | solution.py:379
  20.2 51.5 %gather_kv.1 = (bf16[8,2,64,512]{3,2,1,0:T(8,128)(2,1)}, bf16[8,2,64,512]{3,2,1,0:T(8,128)(2,1)}, bf16[8,128,512]{2,1,0:T(8,128)(2,1)}) custom-call(bf16[2,64,512]{2,1,0:T(8,128)(2,1)} %copy_bitcast_fusion.k_ref, bf16[2,64,512]{2,1,0:T(8,128)(2,1)} %fusion.11.v_ref, bf16[128,4096]{1,0:T(8,128)(2,1)} %fusion.6.a_ref), custom_call_target="tpu_custom_call" | custom-call | tf_op jit(solution)/shard_map/gather_kv/pallas_call | solution.py:143
  71.8 0.7 copy.15.qpos_ref
  72.5 0.7 add.76.kpos_ref
  73.1 0.0 copy-start.5
  73.1 10.6 %attention.1 = (bf16[2,64,2048]{2,1,0:T(8,128)(2,1)}, bf16[2,64,2048]{2,1,0:T(8,128)(2,1)}, bf16[8,2,64,512]{3,2,1,0:T(8,128)(2,1)}, bf16[8,2,64,512]{3,2,1,0:T(8,128)(2,1)}) custom-call(bf16[2,64,2048]{2,1,0:T(8,128)(2,1)} %q_ref.1, bf16[2,64,2048]{2,1,0:T(8,128)(2,1)} %g_ref.1, bf16[8,2,64,512]{3,2,1,0:T(8,128)(2,1)} %get-tuple-element.15.k_ref, ...), custom_call_target="tpu_custom_call" | custom-call | tf_op jit(solution)/shard_map/attention/pallas_call | solution.py:198
  83.7 64.5 %reduce_kv.1 = (bf16[8,2,64,512]{3,2,1,0:T(8,128)(2,1)}, bf16[8,2,64,512]{3,2,1,0:T(8,128)(2,1)}) custom-call(bf16[8,2,64,512]{3,2,1,0:T(8,128)(2,1)} %get-tuple-element.19.dk, bf16[8,2,64,512]{3,2,1,0:T(8,128)(2,1)} %get-tuple-element.20.dv, f32[64,128]{1,0:T(8,128)} %copy-done.2, f32[64,128]{1,0:T(8,128)} %get-tuple-element.29.sin_ref), custom_call_target="tpu_custom_call" | custom-call | tf_op jit(solution)/shard_map/reduce_kv/pallas_call | solution.py:279
  148.2 0.0 copy-done.5
  148.2 0.0 copy-start.4
  148.3 2.1 %convolution_convert_fusion.1 = bf16[512,512]{0,1:T(8,128)(2,1)S(1)} fusion(bf16[1024,512]{1,0:T(8,128)(2,1)S(1)} %bitcast.61, bf16[1024,512]{1,0:T(8,128)(2,1)} %bitcast.59), kind=kOutput, calls=%fused_computation.18 | convolution fusion | flops 537133056 | bytes 2621440 | tf_op jit(solution)/shard_map/dot_general | solution.py:399
  150.3 0.0 copy-done.4
  150.3 0.7 convolution_convert_fusion
  151.1 0.1 pad_maximum_fusion
  151.2 1.3 copy.16
  152.5 12.2 %scatter_weights.1 = f32[128,1024]{1,0:T(8,128)} custom-call(bf16[4,128,1024]{2,1,0:T(8,128)(2,1)} %bitcast.55), custom_call_target="tpu_custom_call" | custom-call | tf_op jit(solution)/shard_map/scatter_weights/pallas_call | solution.py:342
  164.7 2.0 %add_reduce_fusion = (f32[128]{0:T(128)S(1)}, f32[128,512]{1,0:T(8,128)}, f32[128,512]{1,0:T(8,128)}) fusion(bf16[4096,512]{1,0:T(8,128)(2,1)} %param.13, s32[]{:T(128)S(6)} %select_n.26, bf16[4096,512]{1,0:T(8,128)(2,1)} %param.12, f32[128,1024]{1,0:T(8,128)} %scatter_weights.1), kind=kLoop, calls=%fused_computation.26 | loop fusion | flops 393088 | bytes 1311236 | tf_op jit(solution)/shard_map/reduce_sum | solution.py:414
  166.7 0.6 dynamic-slice_divide_fusion
  167.3 0.9 constant_dynamic-slice_fusion
  168.2 0.0 copy-start.1
  168.3 3.8 %fusion.25 = f32[128,4096]{1,0:T(8,128)S(1)} fusion(bf16[128,512]{1,0:T(8,128)(2,1)S(1)} %bitcast.58, bf16[4096,512]{1,0:T(8,128)(2,1)} %param.12), kind=kOutput, calls=%fused_computation.48 | convolution fusion | flops 536870912 | bytes 6422528 | tf_op jit(solution)/shard_map/dot_general | solution.py:390
  172.1 0.0 copy-done.1
  172.1 1.6 fusion.10
  173.7 1.6 fusion.9
  (5 shorter events, 0.0 us)
Async XLA Ops:
  2.5 12.0 %copy-start.2 = (f32[64,128]{1,0:T(8,128)}, f32[64,128]{1,0:T(8,128)S(1)}, u32[]{:S(2)}) copy-start(f32[64,128]{1,0:T(8,128)S(1)} %get-tuple-element.31.cos_ref) | copy-start | bytes 98308
  4.0 6.5 %copy-start = (bf16[2,64,4096]{2,1,0:T(8,128)(2,1)S(1)}, bf16[2,64,4096]{2,1,0:T(8,128)(2,1)}, u32[]{:S(2)}) copy-start(bf16[2,64,4096]{2,1,0:T(8,128)(2,1)} %param.7) | copy-start | bytes 3145732
  4.0 6.5 %copy-start.3 = (f32[4096]{0:T(1024)S(1)}, f32[4096]{0:T(1024)}, u32[]{:S(2)}) copy-start(f32[4096]{0:T(1024)} %param.11) | copy-start | bytes 49156
  73.1 75.1 %copy-start.5 = (bf16[8,128,512]{2,1,0:T(8,128)(2,1)S(1)}, bf16[8,128,512]{2,1,0:T(8,128)(2,1)}, u32[]{:S(2)}) copy-start(bf16[8,128,512]{2,1,0:T(8,128)(2,1)} %get-tuple-element.23) | copy-start | bytes 3145732
  148.2 2.1 %copy-start.4 = (bf16[8,2,64,512]{3,2,1,0:T(8,128)(2,1)S(1)}, bf16[8,2,64,512]{3,2,1,0:T(8,128)(2,1)}, u32[]{:S(2)}) copy-start(bf16[8,2,64,512]{3,2,1,0:T(8,128)(2,1)} %get-tuple-element.22) | copy-start | bytes 3145732
  168.2 3.8 %copy-start.1 = (bf16[4096,512]{1,0:T(8,128)(2,1)S(1)}, bf16[4096,512]{1,0:T(8,128)(2,1)}, u32[]{:S(2)}) copy-start(bf16[4096,512]{1,0:T(8,128)(2,1)} %param.13) | copy-start | bytes 12582916

commit v2 on v1

--- a/solution.py
+++ b/solution.py
@@ -60,65 +60,117 @@
     pl.semaphore_wait(barrier, n - 1)
 
 
-def ring_gather(n, me, firsts, alls, send, recv, extra=None):
+def ring_hops(n, d, t):
+    return n // 2 if d == t else n // 2 - 1
+
+
+def ring_gather(n, me, firsts, alls, send, recv, extra):
     place = ring_place(me, n)
     sign = (1, -1)
     targets = [ring_index(place + 1, n), ring_index(place - 1, n)]
     chunks = firsts[0].shape[0]
-
-    def copy(d, c, s, first=False):
+    lanes = [(c, t, d) for c in range(chunks) for t in range(2) for d in range(2)]
+
+    def copy(d, t, c, s):
         owner = ring_index(place - sign[d] * s, n)
-        src = firsts[d].at[c] if first else alls[d].at[owner, c]
+        src = firsts[t].at[c] if s == 0 else alls[t].at[owner, c]
         return remote(
-            src, alls[d].at[owner, c], send.at[d, c, s], recv.at[d, c, s], "ctx", targets[d]
+            src,
+            alls[t].at[owner, c],
+            send.at[d, t, c, s],
+            recv.at[d, t, c, s],
+            "ctx",
+            targets[d],
         )
 
-    def arrive(d, c, s):
+    def arrive(d, t, c, s):
         owner = ring_index(place - sign[d] * (s + 1), n)
-        slot = alls[d].at[owner, c]
-        remote(slot, slot, send.at[d, c, s], recv.at[d, c, s], "ctx", targets[d]).wait_recv()
-
-    for c in range(chunks):
-        for d in range(2):
-            copy(d, c, 0, first=True).start()
-
-    def step(s, carry):
-        for c in range(chunks):
-            for d in range(2):
-                arrive(d, c, s)
-                copy(d, c, s + 1).start()
-        if extra is not None:
-            extra(s + 1)
-        return carry
-
-    if extra is not None:
-        extra(0)
-    lax.fori_loop(0, n - 2, step, 0)
-    for c in range(chunks):
-        for d in range(2):
-            arrive(d, c, n - 2)
-
-    def drain(s, carry):
-        for c in range(chunks):
-            for d in range(2):
-                copy(d, c, s).wait_send()
-        return carry
-
-    lax.fori_loop(0, n - 1, drain, 0)
-
-
-def gather_kernel(n, k_ref, v_ref, a_ref, gk, gv, ga, send, recv, asend, arecv):
+        slot = alls[t].at[owner, c]
+        remote(
+            slot, slot, send.at[d, t, c, s], recv.at[d, t, c, s], "ctx", targets[d]
+        ).wait_recv()
+
+    for s in range(n // 2):
+        for c, t, d in lanes:
+            if s < ring_hops(n, d, t):
+                if s > 0:
+                    arrive(d, t, c, s - 1)
+                copy(d, t, c, s).start()
+        extra(s)
+    for c, t, d in lanes:
+        hops = ring_hops(n, d, t)
+        arrive(d, t, c, hops - 1)
+    for s in range(n // 2):
+        for c, t, d in lanes:
+            if s < ring_hops(n, d, t):
+                copy(d, t, c, s).wait_send()
+
+
+def load_weights(sources, targets, sems):
+    pieces = sems.shape[1]
+    rows = sources[0].shape[0] // pieces
+    return [
+        [
+            pltpu.make_async_copy(
+                sources[t].at[pl.ds(q * rows, rows)],
+                targets[t].at[pl.ds(q * rows, rows)],
+                sems.at[t, q],
+            )
+            for t in range(2)
+        ]
+        for q in range(pieces)
+    ]
+
+
+PIECES = 4
+
+
+def gather_kernel(
+    n,
+    early,
+    x_ref,
+    gain_ref,
+    wk_hbm,
+    wv_hbm,
+    cos_ref,
+    sin_ref,
+    gk,
+    gv,
+    ga,
+    wk,
+    wv,
+    normed,
+    own_k,
+    own_v,
+    wsem,
+    send,
+    recv,
+    asend,
+    arecv,
+):
     me = lax.axis_index("ctx")
     width = ga.shape[2]
+    seqs, rows, kv_width = own_k.shape
+    model_width = x_ref.shape[1]
+    piece_width = model_width // PIECES
+    loads = load_weights((wk_hbm, wv_hbm), (wk, wv), wsem)
+    for pair in loads:
+        for load in pair:
+            load.start()
+    total = jnp.zeros((x_ref.shape[0], 1), F32)
+    for q in range(PIECES):
+        wide = x_ref[:, q * piece_width : (q + 1) * piece_width].astype(F32)
+        total = total + jnp.sum(wide * wide, axis=1, keepdims=True)
+    rms = lax.rsqrt(total / model_width + EPSILON)
+    for q in range(PIECES):
+        at = slice(q * piece_width, (q + 1) * piece_width)
+        normed[:, at] = (x_ref[:, at].astype(F32) * rms * gain_ref[:, at]).astype(BF16)
     greet("ctx", n, me)
-    gk[me] = k_ref[...]
-    gv[me] = v_ref[...]
-    ga[me] = a_ref[:, pl.ds(pl.multiple_of(me * width, 128), width)]
 
     def piece(j):
         target = (me + j) % n
         return remote(
-            a_ref.at[:, pl.ds(pl.multiple_of(target * width, 128), width)],
+            normed.at[:, pl.ds(pl.multiple_of(target * width, 128), width)],
             ga.at[me],
             asend.at[j - 1],
             arecv.at[j - 1],
@@ -126,32 +178,67 @@
             target,
         )
 
-    ring_gather(n, me, (k_ref, v_ref), (gk, gv), send, recv, lambda s: piece(s + 1).start())
-
-    def finish(j, carry):
+    for j in range(1, 1 + early):
+        piece(j).start()
+    key = jnp.zeros((seqs * rows, kv_width), F32)
+    value = jnp.zeros((seqs * rows, kv_width), F32)
+    for q in range(PIECES):
+        at = slice(q * piece_width, (q + 1) * piece_width)
+        for load in loads[q]:
+            load.wait()
+        part = normed[:, at]
+        key = key + jnp.dot(part, wk[at], preferred_element_type=F32)
+        value = value + jnp.dot(part, wv[at], preferred_element_type=F32)
+    for c in range(seqs):
+        for h in range(kv_width // HEAD_DIM):
+            at = slice(h * HEAD_DIM, (h + 1) * HEAD_DIM)
+            head = key[c * rows : (c + 1) * rows, at]
+            turned = pltpu.roll(head, HEAD_DIM // 2, 1)
+            own_k[c, :, at] = (head * cos_ref[...] + turned * sin_ref[...]).astype(BF16)
+        own_v[c] = value[c * rows : (c + 1) * rows].astype(BF16)
+
+    later = list(range(1 + early, n))
+    half = n // 2
+
+    def extra(s):
+        if s == 0:
+            gk[me] = own_k[...]
+            gv[me] = own_v[...]
+            ga[me] = normed[:, pl.ds(pl.multiple_of(me * width, 128), width)]
+        for i, j in enumerate(later):
+            if i * half // len(later) == s:
+                piece(j).start()
+
+    ring_gather(n, me, (own_k, own_v), (gk, gv), send, recv, extra)
+    for j in range(1, n):
         piece(j).wait_send()
         slot = ga.at[(me + n - j) % n]
         remote(slot, slot, asend.at[j - 1], arecv.at[j - 1], "ctx", (me + j) % n).wait_recv()
-        return carry
-
-    lax.fori_loop(1, n, finish, 0)
-
-
-def gather(n, keys, values, normed):
-    seqs = keys.shape[0]
-    kv = jax.ShapeDtypeStruct((n,) + keys.shape, BF16)
+
+
+ANY = pl.BlockSpec(memory_space=pl.ANY)
+
+
+def gather(n, tokens, norm_gain, key_weight, value_weight, cosine, sine, seqs):
+    count, model_width = tokens.shape
+    rows = count // seqs
+    kv_width = key_weight.shape[1]
+    kv = jax.ShapeDtypeStruct((n, seqs, rows, kv_width), BF16)
+    sems = pltpu.SemaphoreType.DMA((2, 2, seqs, n // 2))
     return pl.pallas_call(
-        functools.partial(gather_kernel, n),
-        out_shape=(
-            kv,
-            kv,
-            jax.ShapeDtypeStruct((n, normed.shape[0], normed.shape[1] // n), BF16),
-        ),
-        in_specs=[VMEM] * 3,
+        functools.partial(gather_kernel, n, n // 2 - 1),
+        out_shape=(kv, kv, jax.ShapeDtypeStruct((n, count, model_width // n), BF16)),
+        in_specs=[VMEM, VMEM, ANY, ANY, VMEM, VMEM],
         out_specs=[VMEM] * 3,
         scratch_shapes=[
-            pltpu.SemaphoreType.DMA((2, seqs, n - 1)),
-            pltpu.SemaphoreType.DMA((2, seqs, n - 1)),
+            pltpu.VMEM(key_weight.shape, BF16),
+            pltpu.VMEM(value_weight.shape, BF16),
+            pltpu.VMEM(tokens.shape, BF16),
+            pltpu.VMEM((seqs, rows, kv_width), BF16),
+            pltpu.VMEM((seqs, rows, kv_width), BF16),
+            pltpu.SemaphoreType.DMA((2, PIECES)),
+            sems,
+            sems,
             pltpu.SemaphoreType.DMA((n - 1,)),
             pltpu.SemaphoreType.DMA((n - 1,)),
         ],
@@ -159,7 +246,7 @@
             collective_id=0, has_side_effects=True, vmem_limit_bytes=LIMIT
         ),
         name="gather_kv",
-    )(keys, values, normed)
+    )(tokens, norm_gain, key_weight, value_weight, cosine, sine)
 
 
 def attention_kernel(q_ref, g_ref, k_ref, v_ref, qpos_ref, kpos_ref, att, dq, dk, dv):
@@ -218,74 +305,154 @@
     )(queries, grads, all_keys, all_values, query_pos[:, None], key_pos[None, :])
 
 
-def reduce_kernel(n, dk, dv, cos_ref, sin_ref, gk, gv, ik, iv, own_k, own_v, rs, rr, send, recv):
+def reduce_kernel(
+    n,
+    dk,
+    dv,
+    cos_ref,
+    sin_ref,
+    x_ref,
+    gain_ref,
+    wk_hbm,
+    wv_hbm,
+    gk,
+    gv,
+    gx,
+    wk,
+    wv,
+    normed_grad,
+    inbox,
+    own_k,
+    own_v,
+    wsem,
+    rs,
+    rr,
+    send,
+    recv,
+):
     me = lax.axis_index("ctx")
     place = ring_place(me, n)
-    seqs = dk.shape[1]
+    _, seqs, rows, kv_width = dk.shape
+    count, model_width = x_ref.shape
+    piece_width = model_width // PIECES
     sign = (1, -1)
     targets = [ring_index(place + 1, n), ring_index(place - 1, n)]
     terms = (dk, dv)
-    inbox = (ik, iv)
+    loads = load_weights((wk_hbm, wv_hbm), (wk, wv), wsem)
+    for pair in loads:
+        for load in pair:
+            load.start()
     greet("ctx", n, me)
-
-    def copy(d, c, s, first=False):
-        src = terms[d].at[targets[1 - d], c] if first else inbox[d].at[s - 1, c]
-        return remote(src, inbox[d].at[s, c], rs.at[d, c, s], rr.at[d, c, s], "ctx", targets[d])
-
-    def total(d, c, s):
-        slot = inbox[d].at[s, c]
-        remote(slot, slot, rs.at[d, c, s], rr.at[d, c, s], "ctx", targets[d]).wait_recv()
-        owner = ring_index(place - sign[d] * (s + 2), n)
-        return inbox[d][s, c].astype(F32) + terms[d][owner, c].astype(F32)
+    lanes = [(c, t, d) for c in range(seqs) for t in range(2) for d in range(2)]
+
+    def copy(d, t, c, s):
+        owner = ring_index(place + sign[d] * ring_hops(n, d, t), n)
+        src = terms[t].at[owner, c] if s == 0 else inbox.at[d, t, s - 1, c]
+        return remote(
+            src,
+            inbox.at[d, t, s, c],
+            rs.at[d, t, c, s],
+            rr.at[d, t, c, s],
+            "ctx",
+            targets[d],
+        )
+
+    def arrive(d, t, c, s):
+        slot = inbox.at[d, t, s, c]
+        remote(slot, slot, rs.at[d, t, c, s], rr.at[d, t, c, s], "ctx", targets[d]).wait_recv()
+
+    for s in range(n // 2):
+        for c, t, d in lanes:
+            hops = ring_hops(n, d, t)
+            if s < hops:
+                if s > 0:
+                    arrive(d, t, c, s - 1)
+                    owner = ring_index(place + sign[d] * (hops - s), n)
+                    inbox[d, t, s - 1, c] = (
+                        inbox[d, t, s - 1, c].astype(F32) + terms[t][owner, c].astype(F32)
+                    ).astype(BF16)
+                copy(d, t, c, s).start()
+
+    def total(t, c):
+        result = terms[t][me, c].astype(F32)
+        for d in (1 - t, t):
+            last = ring_hops(n, d, t) - 1
+            arrive(d, t, c, last)
+            result = result + inbox[d, t, last, c].astype(F32)
+        return result
 
     for c in range(seqs):
-        for d in range(2):
-            copy(d, c, 0, first=True).start()
-
-    def step(s, carry):
-        for c in range(seqs):
-            for d in range(2):
-                inbox[d][s, c] = total(d, c, s).astype(BF16)
-                copy(d, c, s + 1).start()
-        return carry
-
-    lax.fori_loop(0, n - 2, step, 0)
-    for c in range(seqs):
-        key_grad = total(0, c, n - 2)
-        for h in range(key_grad.shape[1] // HEAD_DIM):
-            part = key_grad[:, h * HEAD_DIM : (h + 1) * HEAD_DIM]
-            turned = pltpu.roll(part, HEAD_DIM // 2, 1)
-            back = (part * cos_ref[...] + turned * sin_ref[...]).astype(BF16)
-            own_k[c, :, h * HEAD_DIM : (h + 1) * HEAD_DIM] = back
-        own_v[c] = total(1, c, n - 2).astype(BF16)
-    gk[me] = own_k[...]
-    gv[me] = own_v[...]
-    ring_gather(n, me, (own_k, own_v), (gk, gv), send, recv)
-
-    def drain(s, carry):
-        for c in range(seqs):
-            for d in range(2):
-                slot = inbox[d].at[s, c]
-                remote(slot, slot, rs.at[d, c, s], rr.at[d, c, s], "ctx", targets[d]).wait_send()
-        return carry
-
-    lax.fori_loop(0, n - 1, drain, 0)
-
-
-def reduce_gather(n, key_terms, value_terms, cosine, sine_back):
+        key_grad = total(0, c)
+        for h in range(kv_width // HEAD_DIM):
+            at = slice(h * HEAD_DIM, (h + 1) * HEAD_DIM)
+            turned = pltpu.roll(key_grad[:, at], HEAD_DIM // 2, 1)
+            back = key_grad[:, at] * cos_ref[...] + turned * sin_ref[...]
+            own_k[c, :, at] = back.astype(BF16)
+        own_v[c] = total(1, c).astype(BF16)
+
+    state = {}
+
+    def project(q):
+        at = slice(q * piece_width, (q + 1) * piece_width)
+        for load in loads[q]:
+            load.wait()
+        nt = (((1,), (1,)), ((), ()))
+        part = lax.dot_general(
+            own_k[...].reshape(count, kv_width), wk[at], nt, preferred_element_type=F32
+        ) + lax.dot_general(
+            own_v[...].reshape(count, kv_width), wv[at], nt, preferred_element_type=F32
+        )
+        normed_grad[:, at] = part
+        wide = x_ref[:, at].astype(F32)
+        square = jnp.sum(wide * wide, axis=1, keepdims=True)
+        inner = jnp.sum(part * gain_ref[:, at] * wide, axis=1, keepdims=True)
+        state["square"] = state["square"] + square if q else square
+        state["inner"] = state["inner"] + inner if q else inner
+
+    def finish():
+        rms = lax.rsqrt(state["square"] / model_width + EPSILON)
+        slope = rms * rms * rms * (state["inner"] / model_width)
+        for q in range(PIECES):
+            at = slice(q * piece_width, (q + 1) * piece_width)
+            wide = x_ref[:, at].astype(F32)
+            gx[:, at] = (rms * gain_ref[:, at] * normed_grad[:, at] - wide * slope).astype(BF16)
+
+    def extra(s):
+        if s == 0:
+            gk[me] = own_k[...]
+            gv[me] = own_v[...]
+        for q in range(PIECES):
+            if q * (n // 2) // PIECES == s:
+                project(q)
+                if q == PIECES - 1:
+                    finish()
+
+    ring_gather(n, me, (own_k, own_v), (gk, gv), send, recv, extra)
+    for s in range(n // 2):
+        for c, t, d in lanes:
+            if s < ring_hops(n, d, t):
+                copy(d, t, c, s).wait_send()
+
+
+def reduce_gather(
+    n, key_terms, value_terms, cosine, sine, tokens, norm_gain, key_weight, value_weight
+):
     _, seqs, rows, width = key_terms.shape
     kv = jax.ShapeDtypeStruct(key_terms.shape, BF16)
-    sems = pltpu.SemaphoreType.DMA((2, seqs, n - 1))
+    sems = pltpu.SemaphoreType.DMA((2, 2, seqs, n // 2))
     return pl.pallas_call(
         functools.partial(reduce_kernel, n),
-        out_shape=(kv, kv),
-        in_specs=[VMEM] * 4,
-        out_specs=[VMEM] * 2,
+        out_shape=(kv, kv, jax.ShapeDtypeStruct(tokens.shape, BF16)),
+        in_specs=[VMEM] * 6 + [ANY] * 2,
+        out_specs=[VMEM] * 3,
         scratch_shapes=[
-            pltpu.VMEM((n - 1, seqs, rows, width), BF16),
-            pltpu.VMEM((n - 1, seqs, rows, width), BF16),
+            pltpu.VMEM(key_weight.shape, BF16),
+            pltpu.VMEM(value_weight.shape, BF16),
+            pltpu.VMEM(tokens.shape, F32),
+            pltpu.VMEM((2, 2, n // 2, seqs, rows, width), BF16),
             pltpu.VMEM((seqs, rows, width), BF16),
             pltpu.VMEM((seqs, rows, width), BF16),
+            pltpu.SemaphoreType.DMA((2, PIECES)),
             sems,
             sems,
             sems,
@@ -295,7 +462,7 @@
             collective_id=1, has_side_effects=True, vmem_limit_bytes=LIMIT
         ),
         name="reduce_kv",
-    )(key_terms, value_terms, cosine, sine_back)
+    )(key_terms, value_terms, cosine, sine, tokens, norm_gain, key_weight, value_weight)
 
 
 def scatter_kernel(m, part, out, near, held, far, send, recv):
@@ -368,32 +535,24 @@
     cosine, sine = rotation(query_pos, HEAD_DIM)
     signs = jnp.where(jnp.arange(HEAD_DIM) < HEAD_DIM // 2, -1.0, 1.0).astype(F32)
     flat = tokens.reshape(seqs * rows, model_width)
-    widened = flat.astype(F32)
-    rms_scale = lax.rsqrt(jnp.mean(widened * widened, axis=-1, keepdims=True) + EPSILON)
-    normed = (widened * rms_scale * norm_gain).astype(BF16)
-    key_pre = jnp.dot(normed, key_weight, preferred_element_type=F32)
-    key_pre = key_pre.reshape(seqs, rows, kv_width // HEAD_DIM, HEAD_DIM)
-    turned = jnp.roll(key_pre, HEAD_DIM // 2, axis=-1)
-    keys = key_pre * cosine[None, :, None, :] + turned * (sine * signs)[None, :, None, :]
-    keys = keys.reshape(seqs, rows, kv_width).astype(BF16)
-    values = jnp.dot(normed, value_weight, preferred_element_type=F32)
-    values = values.reshape(seqs, rows, kv_width).astype(BF16)
-
-    all_keys, all_values, slices = gather(n, keys, values, normed)
+    row_gain = norm_gain[None, :]
+    all_keys, all_values, slices = gather(
+        n, flat, row_gain, key_weight, value_weight, cosine, sine * signs, seqs
+    )
     attended, dquery, key_terms, value_terms = attention(
         queries, d_attended, all_keys, all_values, query_pos, token_pos
     )
-    key_back, value_back = reduce_gather(n, key_terms, value_terms, cosine, -sine * signs)
-
-    own_key = lax.dynamic_index_in_dim(key_back, me, 0, False).reshape(seqs * rows, kv_width)
-    own_value = lax.dynamic_index_in_dim(value_back, me, 0, False).reshape(seqs * rows, kv_width)
-    normed_grad = jnp.dot(own_key, key_weight.T, preferred_element_type=F32) + jnp.dot(
-        own_value, value_weight.T, preferred_element_type=F32
-    )
-    inner_mean = jnp.mean(normed_grad * norm_gain * widened, axis=-1, keepdims=True)
-    grad_rows = (
-        rms_scale * norm_gain * normed_grad - widened * rms_scale**3 * inner_mean
-    ).astype(BF16)
+    key_back, value_back, grad_rows = reduce_gather(
+        n,
+        key_terms,
+        value_terms,
+        cosine,
+        -sine * signs,
+        flat,
+        row_gain,
+        key_weight,
+        value_weight,
+    )
 
     stacked = slices.reshape(n * seqs * rows, model_width // n)
     weight_key = jnp.dot(

time: 176 us -> 138 us (0.78)
  Pallas kernels: 139 us -> 126 us
  matrix products: 15.6 us -> 2.81 us
  local copies, waits for them, and re-layouts: 10.4 us -> 3.73 us
  other arithmetic: 9.63 us -> 5.09 us
    pallas_call x2, Pallas kernels: 116 us -> 103 us  [the longest x1 53.8 us: reduce_gather(): pl.pallas_call(functools.partial(reduce_kernel, n), out_shape=(kv, kv, ja...]
    dot_general x4 -> x0, matrix products: 12.7 us -> none  [the longest x1 3.81 us: body(): jnp.dot(own_key, key_weight.T, preferred_element_type=F32)]
    dot_general x1 -> x0, local copies, waits for them, and re-layouts: 6.53 us -> none  [body(): key_pre = jnp.dot(normed, key_weight, preferred_element_type=F32)]
    convert_element_type x3 -> x0, other arithmetic: 3.69 us -> none  [the longest x1 1.59 us: body(): grad_rows = (rms_scale * norm_gain * normed_grad - widened * rms_scale **...]
where the time goes in v2:
time: 138 us
  Pallas kernels  126 us (91%)
  other arithmetic  5.09 us (4%)
  local copies, waits for them, and re-layouts  3.73 us (3%)
  matrix products  2.81 us (2%)
    pallas_call x1, Pallas kernels, reduce_gather(): pl.pallas_call(functools.partial(reduce_kernel, n), out_shape=(kv, kv, ja...  53.8 us
    pallas_call x1, Pallas kernels, gather(): pl.pallas_call(functools.partial(gather_kernel, n, n // 2 - 1), out_shape...  49.1 us
    pallas_call x1, Pallas kernels, scatter(): pl.pallas_call(functools.partial(scatter_kernel, m), out_shape=jax.ShapeD...  12.2 us
    pallas_call x1, Pallas kernels, attention(): pl.pallas_call(attention_kernel, grid=(seqs, kv_heads), out_shape=(jax.Sh...  10.5 us

profile of v2, /device:TPU:0, one launch (start us, length us, event | category | flops | bytes accessed | tf_op | source)
XLA Modules:
  0.0 138.0 jit_solution(10190566578272644319)
XLA Ops:
  0.6 0.7 broadcast_multiply_fusion.1
  1.3 0.1 iota_add_fusion
  1.4 0.7 add.46.kpos_ref
  2.0 0.1 add.44
  2.1 0.1 dynamic-slice_bitcast_fusion
  2.2 0.7 copy.13.qpos_ref
  2.9 0.1 broadcast_multiply_fusion
  3.0 0.8 negate_multiply_fusion
  3.8 49.1 %gather_kv.1 = (bf16[8,2,64,512]{3,2,1,0:T(8,128)(2,1)}, bf16[8,2,64,512]{3,2,1,0:T(8,128)(2,1)}, bf16[8,128,512]{2,1,0:T(8,128)(2,1)}) custom-call(bf16[128,4096]{1,0:T(8,128)(2,1)} %bitcast.14, f32[1,4096]{1,0:T(1,128)} %bitcast.17, bf16[4096,512]{1,0:T(8,128)(2,1)} %wk_hbm.3, bf16[4096,512]{1,0:T(8,128)(2,1)} %wv_hbm.3, ...), custom_call_target="tpu_custom_call" | custom-call | tf_op jit(solution)/shard_map/gather_kv/pallas_call | solution.py:228
  53.0 10.5 %attention.1 = (bf16[2,64,2048]{2,1,0:T(8,128)(2,1)}, bf16[2,64,2048]{2,1,0:T(8,128)(2,1)}, bf16[8,2,64,512]{3,2,1,0:T(8,128)(2,1)}, bf16[8,2,64,512]{3,2,1,0:T(8,128)(2,1)}) custom-call(bf16[2,64,2048]{2,1,0:T(8,128)(2,1)} %q_ref.1, bf16[2,64,2048]{2,1,0:T(8,128)(2,1)} %g_ref.1, bf16[8,2,64,512]{3,2,1,0:T(8,128)(2,1)} %get-tuple-element.16.k_ref, ...), custom_call_target="tpu_custom_call" | custom-call | tf_op jit(solution)/shard_map/attention/pallas_call | solution.py:285
  63.4 0.0 copy-start.1
  63.4 53.8 %reduce_kv.1 = (bf16[8,2,64,512]{3,2,1,0:T(8,128)(2,1)}, bf16[8,2,64,512]{3,2,1,0:T(8,128)(2,1)}, bf16[128,4096]{1,0:T(8,128)(2,1)}) custom-call(bf16[8,2,64,512]{3,2,1,0:T(8,128)(2,1)} %get-tuple-element.20.dk, bf16[8,2,64,512]{3,2,1,0:T(8,128)(2,1)} %get-tuple-element.21.dv, f32[64,128]{1,0:T(8,128)} %get-tuple-element.31.cos_ref, ...), custom_call_target="tpu_custom_call" | custom-call | tf_op jit(solution)/shard_map/reduce_kv/pallas_call | solution.py:443
  117.3 0.0 copy-start.2
  117.3 0.0 copy-done.1
  117.3 2.1 %convolution_convert_fusion.1 = bf16[512,512]{0,1:T(8,128)(2,1)S(1)} fusion(bf16[1024,512]{1,0:T(8,128)(2,1)S(1)} %bitcast.19, bf16[1024,512]{1,0:T(8,128)(2,1)} %bitcast.22), kind=kOutput, calls=%fused_computation.1 | convolution fusion | flops 537133056 | bytes 2621440 | tf_op jit(solution)/shard_map/dot_general | solution.py:558
  119.4 0.0 copy-done.2
  119.4 0.7 convolution_convert_fusion
  120.1 0.0 copy-start
  120.1 0.1 pad_maximum_fusion
  120.2 1.3 copy.14
  121.5 12.2 %scatter_weights.1 = f32[128,1024]{1,0:T(8,128)} custom-call(bf16[4,128,1024]{2,1,0:T(8,128)(2,1)} %bitcast.13), custom_call_target="tpu_custom_call" | custom-call | tf_op jit(solution)/shard_map/scatter_weights/pallas_call | solution.py:509
  133.8 2.0 %add_reduce_fusion = (f32[128]{0:T(128)S(1)}, f32[128,512]{1,0:T(8,128)}, f32[128,512]{1,0:T(8,128)}) fusion(bf16[4096,512]{1,0:T(8,128)(2,1)} %wv_hbm.3, s32[]{:T(128)S(6)} %select_n.20, bf16[4096,512]{1,0:T(8,128)(2,1)} %wk_hbm.3, f32[128,1024]{1,0:T(8,128)} %scatter_weights.1), kind=kLoop, calls=%fused_computation.3 | loop fusion | flops 393088 | bytes 1311236 | tf_op jit(solution)/shard_map/reduce_sum | solution.py:573
  135.8 1.3 dynamic-slice_divide_fusion
  137.0 0.0 copy-done
  137.0 1.0 copy.16
  (2 shorter events, 0.0 us)
Async XLA Ops:
  63.4 53.8 %copy-start.1 = (bf16[8,128,512]{2,1,0:T(8,128)(2,1)S(1)}, bf16[8,128,512]{2,1,0:T(8,128)(2,1)}, u32[]{:S(2)}) copy-start(bf16[8,128,512]{2,1,0:T(8,128)(2,1)} %get-tuple-element.23) | copy-start | bytes 3145732
  117.3 2.1 %copy-start.2 = (bf16[8,2,64,512]{3,2,1,0:T(8,128)(2,1)S(1)}, bf16[8,2,64,512]{3,2,1,0:T(8,128)(2,1)}, u32[]{:S(2)}) copy-start(bf16[8,2,64,512]{3,2,1,0:T(8,128)(2,1)} %get-tuple-element.25) | copy-start | bytes 3145732
  120.1 16.9 %copy-start = (bf16[128,4096]{1,0:T(8,128)(2,1)S(1)}, bf16[128,4096]{1,0:T(8,128)(2,1)}, u32[]{:S(2)}) copy-start(bf16[128,4096]{1,0:T(8,128)(2,1)} %get-tuple-element.22) | copy-start | bytes 3145732

commit v3 on v2

--- a/solution.py
+++ b/solution.py
@@ -52,12 +52,17 @@
 
 
 def greet(axis, n, me):
-    barrier = pltpu.get_barrier_semaphore()
     for j in range(1, n):
         pl.semaphore_signal(
-            barrier, inc=1, device_id={axis: (me + j) % n}, device_id_type=MESH
+            pltpu.get_barrier_semaphore(),
+            inc=1,
+            device_id={axis: (me + j) % n},
+            device_id_type=MESH,
         )
-    pl.semaphore_wait(barrier, n - 1)
+
+
+def greeted(n):
+    pl.semaphore_wait(pltpu.get_barrier_semaphore(), n - 1)
 
 
 def ring_hops(n, d, t):
@@ -125,6 +130,37 @@
 PIECES = 4
 
 
+def attend_group(c, h, q_ref, g_ref, k_ref, v_ref, qpos_ref, kpos_ref, att, dq, dk, dv):
+    n, _, rows, kv_width = k_ref.shape
+    head = HEAD_DIM
+    group = q_ref.shape[2] // kv_width
+    scale = head ** (-0.5)
+    at = pl.ds(pl.multiple_of(h * head, head), head)
+    columns = [pl.ds(pl.multiple_of((h * group + i) * head, head), head) for i in range(group)]
+    query = jnp.concatenate([q_ref[c, :, column] for column in columns], axis=0)
+    grad = jnp.concatenate([g_ref[c, :, column] for column in columns], axis=0)
+    key = k_ref[:, c, :, at].reshape(n * rows, head)
+    value = v_ref[:, c, :, at].reshape(n * rows, head)
+    nt = (((1,), (1,)), ((), ()))
+    nn = (((1,), (0,)), ((), ()))
+    tn = (((0,), (0,)), ((), ()))
+    dot = functools.partial(lax.dot_general, preferred_element_type=F32)
+    keep = kpos_ref[...] <= jnp.concatenate([qpos_ref[...]] * group, axis=0)
+    scores = jnp.where(keep, dot(query, key, nt) * scale, -1e30)
+    exponent = jnp.exp(scores - jnp.max(scores, axis=1, keepdims=True))
+    probability = exponent * (1.0 / jnp.sum(exponent, axis=1, keepdims=True))
+    rounded = probability.astype(BF16)
+    attended = dot(rounded, value, nn).astype(BF16)
+    delta = jnp.sum(grad.astype(F32) * attended.astype(F32), axis=1, keepdims=True)
+    dscores = (probability * (dot(grad, value, nt) - delta)).astype(BF16)
+    dquery = (dot(dscores, key, nn) * scale).astype(BF16)
+    for i in range(group):
+        att[c, :, columns[i]] = attended[i * rows : (i + 1) * rows]
+        dq[c, :, columns[i]] = dquery[i * rows : (i + 1) * rows]
+    dk[:, c, :, at] = (dot(dscores, query, tn) * scale).astype(BF16).reshape(n, rows, head)
+    dv[:, c, :, at] = dot(rounded, grad, tn).astype(BF16).reshape(n, rows, head)
+
+
 def gather_kernel(
     n,
     early,
@@ -134,9 +170,17 @@
     wv_hbm,
     cos_ref,
     sin_ref,
+    q_ref,
+    g_ref,
+    qpos_ref,
+    kpos_ref,
+    ga,
+    att,
+    dq,
+    dk,
+    dv,
     gk,
     gv,
-    ga,
     wk,
     wv,
     normed,
@@ -157,6 +201,7 @@
     for pair in loads:
         for load in pair:
             load.start()
+    greet("ctx", n, me)
     total = jnp.zeros((x_ref.shape[0], 1), F32)
     for q in range(PIECES):
         wide = x_ref[:, q * piece_width : (q + 1) * piece_width].astype(F32)
@@ -165,7 +210,7 @@
     for q in range(PIECES):
         at = slice(q * piece_width, (q + 1) * piece_width)
         normed[:, at] = (x_ref[:, at].astype(F32) * rms * gain_ref[:, at]).astype(BF16)
-    greet("ctx", n, me)
+    greeted(n)
 
     def piece(j):
         target = (me + j) % n
@@ -205,11 +250,18 @@
             gk[me] = own_k[...]
             gv[me] = own_v[...]
             ga[me] = normed[:, pl.ds(pl.multiple_of(me * width, 128), width)]
-        for i, j in enumerate(later):
-            if i * half // len(later) == s:
+        if s == half - 1:
+            for j in later:
                 piece(j).start()
 
     ring_gather(n, me, (own_k, own_v), (gk, gv), send, recv, extra)
+    kv_heads = kv_width // HEAD_DIM
+
+    def attend(i, carry):
+        attend_group(i // kv_heads, i % kv_heads, q_ref, g_ref, gk, gv, qpos_ref, kpos_ref, att, dq, dk, dv)
+        return carry
+
+    lax.fori_loop(0, seqs * kv_heads, attend, 0)
     for j in range(1, n):
         piece(j).wait_send()
         slot = ga.at[(me + n - j) % n]
@@ -219,18 +271,26 @@
 ANY = pl.BlockSpec(memory_space=pl.ANY)
 
 
-def gather(n, tokens, norm_gain, key_weight, value_weight, cosine, sine, seqs):
+def gather_attend(n, tokens, norm_gain, key_weight, value_weight, cosine, sine, queries, grads, query_pos, key_pos):
     count, model_width = tokens.shape
-    rows = count // seqs
+    seqs, rows, _ = queries.shape
     kv_width = key_weight.shape[1]
-    kv = jax.ShapeDtypeStruct((n, seqs, rows, kv_width), BF16)
+    kv = (n, seqs, rows, kv_width)
     sems = pltpu.SemaphoreType.DMA((2, 2, seqs, n // 2))
     return pl.pallas_call(
         functools.partial(gather_kernel, n, n // 2 - 1),
-        out_shape=(kv, kv, jax.ShapeDtypeStruct((n, count, model_width // n), BF16)),
-        in_specs=[VMEM, VMEM, ANY, ANY, VMEM, VMEM],
-        out_specs=[VMEM] * 3,
+        out_shape=(
+            jax.ShapeDtypeStruct((n, count, model_width // n), BF16),
+            jax.ShapeDtypeStruct(queries.shape, BF16),
+            jax.ShapeDtypeStruct(queries.shape, BF16),
+            jax.ShapeDtypeStruct(kv, BF16),
+            jax.ShapeDtypeStruct(kv, BF16),
+        ),
+        in_specs=[VMEM, VMEM, ANY, ANY] + [VMEM] * 6,
+        out_specs=[VMEM] * 5,
         scratch_shapes=[
+            pltpu.VMEM(kv, BF16),
+            pltpu.VMEM(kv, BF16),
             pltpu.VMEM(key_weight.shape, BF16),
             pltpu.VMEM(value_weight.shape, BF16),
             pltpu.VMEM(tokens.shape, BF16),
@@ -245,64 +305,19 @@
         compiler_params=pltpu.CompilerParams(
             collective_id=0, has_side_effects=True, vmem_limit_bytes=LIMIT
         ),
-        name="gather_kv",
-    )(tokens, norm_gain, key_weight, value_weight, cosine, sine)
-
-
-def attention_kernel(q_ref, g_ref, k_ref, v_ref, qpos_ref, kpos_ref, att, dq, dk, dv):
-    n, _, rows, head = k_ref.shape
-    group = q_ref.shape[2] // head
-    scale = head ** (-0.5)
-    query = jnp.concatenate([q_ref[0, :, i * head : (i + 1) * head] for i in range(group)], axis=0)
-    grad = jnp.concatenate([g_ref[0, :, i * head : (i + 1) * head] for i in range(group)], axis=0)
-    key = k_ref[...].reshape(n * rows, head)
-    value = v_ref[...].reshape(n * rows, head)
-    nt = (((1,), (1,)), ((), ()))
-    nn = (((1,), (0,)), ((), ()))
-    tn = (((0,), (0,)), ((), ()))
-    dot = functools.partial(lax.dot_general, preferred_element_type=F32)
-    keep = kpos_ref[...] <= jnp.concatenate([qpos_ref[...]] * group, axis=0)
-    scores = jnp.where(keep, dot(query, key, nt) * scale, -1e30)
-    exponent = jnp.exp(scores - jnp.max(scores, axis=1, keepdims=True))
-    probability = exponent * (1.0 / jnp.sum(exponent, axis=1, keepdims=True))
-    rounded = probability.astype(BF16)
-    attended = dot(rounded, value, nn).astype(BF16)
-    delta = jnp.sum(grad.astype(F32) * attended.astype(F32), axis=1, keepdims=True)
-    dscores = (probability * (dot(grad, value, nt) - delta)).astype(BF16)
-    dquery = (dot(dscores, key, nn) * scale).astype(BF16)
-    for i in range(group):
-        att[0, :, i * head : (i + 1) * head] = attended[i * rows : (i + 1) * rows]
-        dq[0, :, i * head : (i + 1) * head] = dquery[i * rows : (i + 1) * rows]
-    dk[...] = (dot(dscores, query, tn) * scale).astype(BF16).reshape(n, 1, rows, head)
-    dv[...] = dot(rounded, grad, tn).astype(BF16).reshape(n, 1, rows, head)
-
-
-def attention(queries, grads, all_keys, all_values, query_pos, key_pos):
-    n, seqs, rows, width = all_keys.shape
-    kv_heads = width // HEAD_DIM
-    wide = pl.BlockSpec((1, rows, queries.shape[2] // kv_heads), lambda s, h: (s, 0, h))
-    narrow = pl.BlockSpec((n, 1, rows, HEAD_DIM), lambda s, h: (0, s, 0, h))
-    return pl.pallas_call(
-        attention_kernel,
-        grid=(seqs, kv_heads),
-        out_shape=(
-            jax.ShapeDtypeStruct(queries.shape, BF16),
-            jax.ShapeDtypeStruct(queries.shape, BF16),
-            jax.ShapeDtypeStruct(all_keys.shape, BF16),
-            jax.ShapeDtypeStruct(all_keys.shape, BF16),
-        ),
-        in_specs=[
-            wide,
-            wide,
-            narrow,
-            narrow,
-            pl.BlockSpec((rows, 1), lambda s, h: (0, 0)),
-            pl.BlockSpec((1, n * rows), lambda s, h: (0, 0)),
-        ],
-        out_specs=[wide, wide, narrow, narrow],
-        compiler_params=pltpu.CompilerParams(vmem_limit_bytes=LIMIT),
-        name="attention",
-    )(queries, grads, all_keys, all_values, query_pos[:, None], key_pos[None, :])
+        name="gather_attend",
+    )(
+        tokens,
+        norm_gain,
+        key_weight,
+        value_weight,
+        cosine,
+        sine,
+        queries,
+        grads,
+        query_pos[:, None],
+        key_pos[None, :],
+    )
 
 
 def reduce_kernel(
@@ -343,6 +358,7 @@
         for load in pair:
             load.start()
     greet("ctx", n, me)
+    greeted(n)
     lanes = [(c, t, d) for c in range(seqs) for t in range(2) for d in range(2)]
 
     def copy(d, t, c, s):
@@ -465,7 +481,7 @@
     )(key_terms, value_terms, cosine, sine, tokens, norm_gain, key_weight, value_weight)
 
 
-def scatter_kernel(m, part, out, near, held, far, send, recv):
+def scatter_kernel(m, x_ref, k_ref, v_ref, out, part, near, held, far, send, recv):
     me = lax.axis_index("dp")
     greet("dp", m, me)
     half = m // 2
@@ -482,9 +498,27 @@
         at = half + j - 1
         return remote(held.at[j - 1], far.at[j - 1], send.at[at], recv.at[at], "dp", to)
 
+    count, kv_width = k_ref.shape[0] * k_ref.shape[1], k_ref.shape[2]
+    rows = out.shape[0]
+
+    def multiply(t):
+        at = pl.ds(pl.multiple_of(t * rows, 128), rows)
+        lhs = x_ref[:, :, at].reshape(count, rows)
+        for ref, start in ((k_ref, 0), (v_ref, kv_width)):
+            rhs = ref[...].reshape(count, kv_width)
+            term = lax.dot_general(
+                lhs, rhs, (((0,), (0,)), ((), ())), preferred_element_type=F32
+            )
+            part[t, :, start : start + kv_width] = term.astype(BF16)
+
     order = list(range(1, half)) + [0]
+    for i, j in enumerate(order):
+        multiply(2 * ((me // 2 + j) % half) + pair % 2)
+        if i == 0:
+            greeted(m)
+        first(j).start()
     for j in order:
-        first(j).start()
+        multiply(2 * ((me // 2 + j) % half) + me % 2)
     for j in order:
         to = (me // 2 + j) % half
         first(j).wait_recv()
@@ -503,15 +537,16 @@
         second(j).wait_send()
 
 
-def scatter(m, part):
-    _, rows, width = part.shape
+def scatter(m, slices, key_back, value_back):
+    rows, width = slices.shape[2] // m, 2 * key_back.shape[2]
     half = m // 2
     return pl.pallas_call(
         functools.partial(scatter_kernel, m),
         out_shape=jax.ShapeDtypeStruct((rows, width), F32),
-        in_specs=[VMEM],
+        in_specs=[VMEM] * 3,
         out_specs=VMEM,
         scratch_shapes=[
+            pltpu.VMEM((m, rows, width), BF16),
             pltpu.VMEM((half, rows, width), BF16),
             pltpu.VMEM((max(half - 1, 1), rows, width), BF16),
             pltpu.VMEM((max(half - 1, 1), rows, width), BF16),
@@ -522,7 +557,7 @@
             collective_id=2, has_side_effects=True, vmem_limit_bytes=LIMIT
         ),
         name="scatter_weights",
-    )(part)
+    )(slices, key_back, value_back)
 
 
 def body(n, m, tokens, queries, d_attended, span_order, norm_gain, key_weight, value_weight):
@@ -536,11 +571,18 @@
     signs = jnp.where(jnp.arange(HEAD_DIM) < HEAD_DIM // 2, -1.0, 1.0).astype(F32)
     flat = tokens.reshape(seqs * rows, model_width)
     row_gain = norm_gain[None, :]
-    all_keys, all_values, slices = gather(
-        n, flat, row_gain, key_weight, value_weight, cosine, sine * signs, seqs
-    )
-    attended, dquery, key_terms, value_terms = attention(
-        queries, d_attended, all_keys, all_values, query_pos, token_pos
+    slices, attended, dquery, key_terms, value_terms = gather_attend(
+        n,
+        flat,
+        row_gain,
+        key_weight,
+        value_weight,
+        cosine,
+        sine * signs,
+        queries,
+        d_attended,
+        query_pos,
+        token_pos,
     )
     key_back, value_back, grad_rows = reduce_gather(
         n,
@@ -554,16 +596,14 @@
         value_weight,
     )
 
-    stacked = slices.reshape(n * seqs * rows, model_width // n)
-    weight_key = jnp.dot(
-        stacked.T, key_back.reshape(n * seqs * rows, kv_width), preferred_element_type=F32
-    )
-    weight_value = jnp.dot(
-        stacked.T, value_back.reshape(n * seqs * rows, kv_width), preferred_element_type=F32
+    count = seqs * rows
+    summed = scatter(
+        m,
+        slices,
+        key_back.reshape(n, count, kv_width),
+        value_back.reshape(n, count, kv_width),
     )
     own_rows = model_width // (n * m)
-    part = jnp.concatenate([weight_key.astype(BF16), weight_value.astype(BF16)], axis=1)
-    summed = scatter(m, part.reshape(m, own_rows, 2 * kv_width))
     grad_key_weight = summed[:, :kv_width]
     grad_value_weight = summed[:, kv_width:]
     start = (me * m + dp) * own_rows

time: 138 us -> 131 us (0.949)
  Pallas kernels: 126 us -> 121 us
  matrix products: 2.81 us -> 0 us
    pallas_call x2 -> x1, Pallas kernels: 59.6 us -> 47.5 us  [gather_attend(): pl.pallas_call(functools.partial(gather_kernel, n, n // 2 - 1), out_shape...]
    pallas_call x1, Pallas kernels: 53.8 us -> 60.1 us  [reduce_gather(): pl.pallas_call(functools.partial(reduce_kernel, n), out_shape=(kv, kv, ja...]
    dot_general x2 -> x0, matrix products: 2.81 us -> none  [the longest x1 2.06 us: body(): jnp.dot(stacked.T, key_back.reshape(n * seqs * rows, kv_width), preferred...]
    unnamed x7 -> x9, local copies, waits for them, and re-layouts: 0.98 us -> 2.57 us
where the time goes in v3:
time: 131 us; the launch traced here: 130 us
  Pallas kernels  121 us (92%)
  other arithmetic  5.02 us (4%)
  local copies, waits for them, and re-layouts  4.02 us (3%)
    pallas_call x1, Pallas kernels, reduce_gather(): pl.pallas_call(functools.partial(reduce_kernel, n), out_shape=(kv, kv, ja...  60.1 us
    pallas_call x1, Pallas kernels, gather_attend(): pl.pallas_call(functools.partial(gather_kernel, n, n // 2 - 1), out_shape...  47.5 us
    pallas_call x1, Pallas kernels, scatter(): pl.pallas_call(functools.partial(scatter_kernel, m), out_shape=jax.ShapeD...  13 us

profile of v3, /device:TPU:0, one launch (start us, length us, event | category | flops | bytes accessed | tf_op | source)
XLA Modules:
  0.0 130.3 jit_solution(13743661607901706103)
XLA Ops:
  0.6 0.7 broadcast_multiply_fusion.1
  1.3 0.1 iota_add_fusion
  1.4 0.7 add.46.kpos_ref
  2.0 0.1 add.44
  2.1 0.1 dynamic-slice_bitcast_fusion
  2.2 0.7 copy.13.qpos_ref
  2.9 0.1 broadcast_multiply_fusion
  3.0 0.8 negate_multiply_fusion
  3.8 47.5 %gather_attend.1 = (bf16[8,128,512]{2,1,0:T(8,128)(2,1)}, bf16[2,64,2048]{2,1,0:T(8,128)(2,1)}, bf16[2,64,2048]{2,1,0:T(8,128)(2,1)}, bf16[8,2,64,512]{3,2,1,0:T(8,128)(2,1)}, bf16[8,2,64,512]{3,2,1,0:T(8,128)(2,1)}) custom-call(bf16[128,4096]{1,0:T(8,128)(2,1)} %bitcast.7, f32[1,4096]{1,0:T(1,128)} %bitcast.12, bf16[4096,512]{1,0:T(8,128)(2,1)} %wk_hbm.3, ...), custom_call_target="tpu_custom_call" | custom-call | tf_op jit(solution)/shard_map/gather_attend/pallas_call | solution.py:280
  51.4 60.1 %reduce_kv.1 = (bf16[8,2,64,512]{3,2,1,0:T(8,128)(2,1)}, bf16[8,2,64,512]{3,2,1,0:T(8,128)(2,1)}, bf16[128,4096]{1,0:T(8,128)(2,1)}) custom-call(bf16[8,2,64,512]{3,2,1,0:T(8,128)(2,1)} %get-tuple-element.16.dk, bf16[8,2,64,512]{3,2,1,0:T(8,128)(2,1)} %get-tuple-element.17.dv, f32[64,128]{1,0:T(8,128)} %get-tuple-element.27.cos_ref, ...), custom_call_target="tpu_custom_call" | custom-call | tf_op jit(solution)/shard_map/reduce_kv/pallas_call | solution.py:459
  111.5 0.0 copy-start.2
  111.5 0.0 copy-start.1
  111.5 0.0 copy-start
  111.5 13.0 %scatter_weights.1 = f32[128,1024]{1,0:T(8,128)} custom-call(bf16[8,128,512]{2,1,0:T(8,128)(2,1)} %get-tuple-element.19.x_ref, bf16[8,128,512]{2,1,0:T(8,128)(2,1)} %bitcast.9, bf16[8,128,512]{2,1,0:T(8,128)(2,1)} %bitcast.10), custom_call_target="tpu_custom_call" | custom-call | tf_op jit(solution)/shard_map/scatter_weights/pallas_call | solution.py:543
  124.5 2.0 %add_reduce_fusion = (f32[128]{0:T(128)S(1)}, f32[128,512]{1,0:T(8,128)}, f32[128,512]{1,0:T(8,128)}) fusion(bf16[4096,512]{1,0:T(8,128)(2,1)} %wv_hbm.3, s32[]{:T(128)S(6)} %select_n.20, bf16[4096,512]{1,0:T(8,128)(2,1)} %wk_hbm.3, f32[128,1024]{1,0:T(8,128)} %scatter_weights.1), kind=kLoop, calls=%fused_computation | loop fusion | flops 393088 | bytes 1311236 | tf_op jit(solution)/shard_map/reduce_sum | solution.py:613
  126.5 1.3 dynamic-slice_divide_fusion
  127.8 0.0 copy-done.2
  127.8 0.8 copy.17
  128.6 0.0 copy-done.1
  128.6 0.8 copy.18
  129.4 0.0 copy-done
  129.4 1.0 copy.19
  (2 shorter events, 0.0 us)
Async XLA Ops:
  111.5 16.3 %copy-start.2 = (bf16[2,64,2048]{2,1,0:T(8,128)(2,1)S(1)}, bf16[2,64,2048]{2,1,0:T(8,128)(2,1)}, u32[]{:S(2)}) copy-start(bf16[2,64,2048]{2,1,0:T(8,128)(2,1)} %get-tuple-element.36) | copy-start | bytes 1572868
  111.5 17.1 %copy-start.1 = (bf16[2,64,2048]{2,1,0:T(8,128)(2,1)S(1)}, bf16[2,64,2048]{2,1,0:T(8,128)(2,1)}, u32[]{:S(2)}) copy-start(bf16[2,64,2048]{2,1,0:T(8,128)(2,1)} %get-tuple-element.37) | copy-start | bytes 1572868
  111.5 17.9 %copy-start = (bf16[128,4096]{1,0:T(8,128)(2,1)S(1)}, bf16[128,4096]{1,0:T(8,128)(2,1)}, u32[]{:S(2)}) copy-start(bf16[128,4096]{1,0:T(8,128)(2,1)} %get-tuple-element.18) | copy-start | bytes 3145732

commit v4 on v3

--- a/solution.py
+++ b/solution.py
@@ -261,7 +261,7 @@
         attend_group(i // kv_heads, i % kv_heads, q_ref, g_ref, gk, gv, qpos_ref, kpos_ref, att, dq, dk, dv)
         return carry
 
-    lax.fori_loop(0, seqs * kv_heads, attend, 0)
+    lax.fori_loop(0, seqs * kv_heads, attend, 0, unroll=2)
     for j in range(1, n):
         piece(j).wait_send()
         slot = ga.at[(me + n - j) % n]

time: 131 us -> 130 us (level)
  no operation moved by 1% of the time
where the time goes in v4:
time: 130 us
  Pallas kernels  120 us (92%)
  other arithmetic  5.02 us (4%)
  local copies, waits for them, and re-layouts  4.02 us (3%)
    pallas_call x1, Pallas kernels, reduce_gather(): pl.pallas_call(functools.partial(reduce_kernel, n), out_shape=(kv, kv, ja...  60 us
    pallas_call x1, Pallas kernels, gather_attend(): pl.pallas_call(functools.partial(gather_kernel, n, n // 2 - 1), out_shape...  46.9 us
    pallas_call x1, Pallas kernels, scatter(): pl.pallas_call(functools.partial(scatter_kernel, m), out_shape=jax.ShapeD...  13 us

profile of v4, /device:TPU:0, one launch (start us, length us, event | category | flops | bytes accessed | tf_op | source)
XLA Modules:
  0.0 129.6 jit_solution(11670992271659433914)
XLA Ops:
  0.6 0.7 broadcast_multiply_fusion.1
  1.3 0.1 iota_add_fusion
  1.4 0.7 add.46.kpos_ref
  2.0 0.1 add.44
  2.1 0.1 dynamic-slice_bitcast_fusion
  2.2 0.7 copy.13.qpos_ref
  2.9 0.1 broadcast_multiply_fusion
  3.0 0.8 negate_multiply_fusion
  3.8 46.9 %gather_attend.1 = (bf16[8,128,512]{2,1,0:T(8,128)(2,1)}, bf16[2,64,2048]{2,1,0:T(8,128)(2,1)}, bf16[2,64,2048]{2,1,0:T(8,128)(2,1)}, bf16[8,2,64,512]{3,2,1,0:T(8,128)(2,1)}, bf16[8,2,64,512]{3,2,1,0:T(8,128)(2,1)}) custom-call(bf16[128,4096]{1,0:T(8,128)(2,1)} %bitcast.7, f32[1,4096]{1,0:T(1,128)} %bitcast.12, bf16[4096,512]{1,0:T(8,128)(2,1)} %wk_hbm.3, ...), custom_call_target="tpu_custom_call" | custom-call | tf_op jit(solution)/shard_map/gather_attend/pallas_call | solution.py:280
  50.7 60.0 %reduce_kv.1 = (bf16[8,2,64,512]{3,2,1,0:T(8,128)(2,1)}, bf16[8,2,64,512]{3,2,1,0:T(8,128)(2,1)}, bf16[128,4096]{1,0:T(8,128)(2,1)}) custom-call(bf16[8,2,64,512]{3,2,1,0:T(8,128)(2,1)} %get-tuple-element.16.dk, bf16[8,2,64,512]{3,2,1,0:T(8,128)(2,1)} %get-tuple-element.17.dv, f32[64,128]{1,0:T(8,128)} %get-tuple-element.27.cos_ref, ...), custom_call_target="tpu_custom_call" | custom-call | tf_op jit(solution)/shard_map/reduce_kv/pallas_call | solution.py:459
  110.7 0.0 copy-start.2
  110.7 0.0 copy-start.1
  110.7 0.0 copy-start
  110.7 13.0 %scatter_weights.1 = f32[128,1024]{1,0:T(8,128)} custom-call(bf16[8,128,512]{2,1,0:T(8,128)(2,1)} %get-tuple-element.19.x_ref, bf16[8,128,512]{2,1,0:T(8,128)(2,1)} %bitcast.9, bf16[8,128,512]{2,1,0:T(8,128)(2,1)} %bitcast.10), custom_call_target="tpu_custom_call" | custom-call | tf_op jit(solution)/shard_map/scatter_weights/pallas_call | solution.py:543
  123.7 2.0 %add_reduce_fusion = (f32[128]{0:T(128)S(1)}, f32[128,512]{1,0:T(8,128)}, f32[128,512]{1,0:T(8,128)}) fusion(bf16[4096,512]{1,0:T(8,128)(2,1)} %wv_hbm.3, s32[]{:T(128)S(6)} %select_n.20, bf16[4096,512]{1,0:T(8,128)(2,1)} %wk_hbm.3, f32[128,1024]{1,0:T(8,128)} %scatter_weights.1), kind=kLoop, calls=%fused_computation | loop fusion | flops 393088 | bytes 1311236 | tf_op jit(solution)/shard_map/reduce_sum | solution.py:613
  125.7 1.3 dynamic-slice_divide_fusion
  127.0 0.0 copy-done.2
  127.0 0.8 copy.17
  127.8 0.0 copy-done.1
  127.8 0.8 copy.18
  128.6 0.0 copy-done
  128.6 1.0 copy.19
  (2 shorter events, 0.0 us)
Async XLA Ops:
  110.7 16.3 %copy-start.2 = (bf16[2,64,2048]{2,1,0:T(8,128)(2,1)S(1)}, bf16[2,64,2048]{2,1,0:T(8,128)(2,1)}, u32[]{:S(2)}) copy-start(bf16[2,64,2048]{2,1,0:T(8,128)(2,1)} %get-tuple-element.36) | copy-start | bytes 1572868
  110.7 17.1 %copy-start.1 = (bf16[2,64,2048]{2,1,0:T(8,128)(2,1)S(1)}, bf16[2,64,2048]{2,1,0:T(8,128)(2,1)}, u32[]{:S(2)}) copy-start(bf16[2,64,2048]{2,1,0:T(8,128)(2,1)} %get-tuple-element.37) | copy-start | bytes 1572868
  110.7 17.9 %copy-start = (bf16[128,4096]{1,0:T(8,128)(2,1)S(1)}, bf16[128,4096]{1,0:T(8,128)(2,1)}, u32[]{:S(2)}) copy-start(bf16[128,4096]{1,0:T(8,128)(2,1)} %get-tuple-element.18) | copy-start | bytes 3145732
